TPU v7x, 16 devices: a 4x2x1 block of a 4x4x8 slice. The times are simulated.
16 devices in a mesh: rep: 2 (over y, z), dp: 8 (over x, core).
Axes of the slice: x: 4, y: 2, z: 1, core: 2. Of those that a mesh axis runs over, the one named last changes fastest.
The devices are a block of a 4x4x8 slice.
Arguments:
- g_w_gate: bfloat16 [16, 2, 512, 4096], P(('rep', 'dp')), parts along dimension 0
- g_w_up: bfloat16 [16, 2, 512, 4096], P(('rep', 'dp')), parts along dimension 0
- g_w_down: bfloat16 [16, 2, 4096, 512], P(('rep', 'dp')), parts along dimension 0
- w_gate: bfloat16 [2, 512, 4096], replicated
- w_up: bfloat16 [2, 512, 4096], replicated
- w_down: bfloat16 [2, 4096, 512], replicated
- m_w_gate: float32 [2, 512, 4096], P(None, 'dp')
- m_w_up: float32 [2, 512, 4096], P(None, 'dp')
- m_w_down: float32 [2, 4096, 512], P(None, 'dp')
- v_w_gate: float32 [2, 512, 4096], P(None, 'dp')
- v_w_up: float32 [2, 512, 4096], P(None, 'dp')
- v_w_down: float32 [2, 4096, 512], P(None, 'dp')
Outputs:
- output 1: bfloat16 [4, 512, 4096], P('rep'), parts along dimension 0
- output 2: bfloat16 [4, 512, 4096], P('rep'), parts along dimension 0
- output 3: bfloat16 [4, 4096, 512], P('rep'), parts along dimension 0
- output 4: float32 [4, 512, 4096], P('rep', 'dp'), parts along dimension 0
- output 5: float32 [4, 512, 4096], P('rep', 'dp'), parts along dimension 0
- output 6: float32 [4, 4096, 512], P('rep', 'dp'), parts along dimension 0
- output 7: float32 [4, 512, 4096], P('rep', 'dp'), parts along dimension 0
- output 8: float32 [4, 512, 4096], P('rep', 'dp'), parts along dimension 0
- output 9: float32 [4, 4096, 512], P('rep', 'dp'), parts along dimension 0
There are 2 independent parts. A program takes and returns all parts, laid end to end along the dimension named above; an argument that names none is the same for every part.
All inputs are finite; a program needn't handle non-finite values.
Results may differ from a plain program's by a relative error of at most 0.022.
Values are sent between devices in bfloat16 or wider.
A program may use at most 768 MiB of HBM per device.

v0:
```python
import jax
import jax.numpy as jnp
from jax import lax
from jax.sharding import PartitionSpec as P


def adamw(w, m, v, g):
    m = 0.9 * m + 0.1 * g
    v = 0.95 * v + 0.05 * g * g
    step = m * lax.rsqrt(v + 1e-8) + 0.1 * w
    return (w - 0.02 * step).astype(jnp.bfloat16), m, v


def clipped(gradients, sum_of_squares, count):
    factor = jnp.minimum(1.0, 0.5 * lax.rsqrt(sum_of_squares / count + 1e-30))
    return [g * factor for g in gradients]


def solution(mesh):
    def step(*arrays):
        terms, weights, m, v = (arrays[i : i + 3] for i in (0, 3, 6, 9))
        gradients = [lax.psum_scatter(t[0], "dp", scatter_dimension=1, tiled=True).astype(jnp.float32) for t in terms]
        squares = lax.psum(sum(jnp.sum(g * g) for g in gradients), "dp")
        gradients = clipped(gradients, squares, lax.psum(1, "dp") * sum(g.size for g in gradients))
        me = lax.axis_index("dp")
        own = [lax.dynamic_slice_in_dim(w, me * one.shape[1], one.shape[1], 1).astype(jnp.float32) for w, one in zip(weights, m, strict=True)]
        new = [adamw(w, m, v, g) for w, m, v, g in zip(own, m, v, gradients, strict=True)]
        whole = [lax.all_gather(one[0], "dp", axis=1, tiled=True) for one in new]
        return (*whole, *(one[1] for one in new), *(one[2] for one in new))

    all_of, cut = P(None, None, None), P(None, "dp", None)
    return jax.shard_map(
        step,
        mesh=mesh,
        in_specs=(P(("rep", "dp"), None, None, None),) * 3 + (all_of,) * 3 + (cut,) * 6,
        out_specs=(P("rep", None, None),) * 3 + (P("rep", "dp", None),) * 6,
        check_vma=False,
    )
```

profile of v0, /device:TPU:113, one launch (start us, length us, event | category | flops | bytes accessed | tf_op | source)
XLA Modules:
  0.0 355.8 jit_solution(7987578605996707757)
XLA Ops:
  7.3 0.7 reduce-scatter.4.cloned.1.call-update
  8.0 0.1 reduce-scatter.6.cloned.1.call-start
  8.1 0.7 reduce-scatter.6.cloned.1.call-update
  8.8 0.1 reduce-scatter.8.cloned.1.call-start
  8.9 0.7 reduce-scatter.8.cloned.1.call-update
  9.6 0.1 all-gather.8.cloned.1.call-start
  9.7 51.6 %reduce-scatter.4.cloned.1.call-done = bf16[2,64,4096]{2,1,0:T(8,128)(2,1)} async-done(((bf16[2,512,4096]{2,1,0:T(8,128)(2,1)}), bf16[2,64,4096]{2,1,0:T(8,128)(2,1)}) %reduce-scatter.4.cloned.1.call-update) | async-done | bytes 1048592 | tf_op jit(solution)/shard_map/reduce_scatter | solution.py:22
  61.2 2.4 fusion.9
  63.6 48.0 %reduce-scatter.6.cloned.1.call-done = bf16[2,64,4096]{2,1,0:T(8,128)(2,1)} async-done(((bf16[2,512,4096]{2,1,0:T(8,128)(2,1)}), bf16[2,64,4096]{2,1,0:T(8,128)(2,1)}) %reduce-scatter.6.cloned.1.call-update) | async-done | bytes 1048592 | tf_op jit(solution)/shard_map/reduce_scatter | solution.py:22
  111.6 2.4 fusion.10
  115.3 46.7 %reduce-scatter.8.cloned.1.call-done = bf16[2,512,512]{2,1,0:T(8,128)(2,1)} async-done(((bf16[2,4096,512]{2,1,0:T(8,128)(2,1)}), bf16[2,512,512]{2,1,0:T(8,128)(2,1)}) %reduce-scatter.8.cloned.1.call-update) | async-done | bytes 1048592 | tf_op jit(solution)/shard_map/reduce_scatter | solution.py:22
  162.1 2.4 fusion.11
  165.1 13.4 %psum.7 = f32[]{:T(128)} all-reduce(f32[]{:T(128)S(6)} %add.65), channel_id=1, replica_groups=mesh['rep'=2,'dp'=8] {'dp'}, use_global_device_ids=true, to_apply=%region_6.0 | all-reduce | flops 1 | bytes 8 | tf_op jit(solution)/shard_map/psum | solution.py:23
  179.2 6.0 %fusion.17 = (bf16[2,512,512]{2,1,0:T(8,128)(2,1)}, f32[2,512,512]{2,1,0:T(8,128)}, f32[2,512,512]{2,1,0:T(8,128)}) fusion(bf16[2,4096,512]{2,1,0:T(8,128)(2,1)} %param.17, s32[]{:T(128)S(6)} %select_n.8, f32[]{:T(128)S(6)} %min_shard_map.3, bf16[2,512,512]{2,1,0:T(8,128)(2,1)} %reduce-scatter.8.cloned.1.call-done, f32[2,512,512]{2,1,0:T(8,128)} %param.23, ...), kind=kLoop, calls=%fused_computation.32 | loop fusion | flops 8912896 | bytes 11534344 | tf_op jit(solution)/shard_map/convert_element_type | solution.py:11
  185.2 0.1 all-gather.4.cloned.1.call-start
  185.3 5.6 %fusion.8 = (bf16[2,64,4096]{2,1,0:T(8,128)(2,1)}, f32[2,64,4096]{2,1,0:T(8,128)}, f32[2,64,4096]{2,1,0:T(8,128)}) fusion(bf16[2,512,4096]{2,1,0:T(8,128)(2,1)} %param.15, s32[]{:T(128)S(6)} %select_n.7, f32[]{:T(128)S(6)} %min_shard_map.3, bf16[2,64,4096]{2,1,0:T(8,128)(2,1)S(1)} %copy-done.1, f32[2,64,4096]{2,1,0:T(8,128)} %param.21, f32[2,64,4096]{2,1,0:T(8,128)} %param.18), kind=kLoop, calls=%fused_computation.23 | loop fusion | flops 8912896 | bytes 11534344 | tf_op jit(solution)/shard_map/convert_element_type | solution.py:11
  191.0 0.1 all-gather.6.cloned.1.call-start
  191.1 5.5 %fusion.14 = (bf16[2,64,4096]{2,1,0:T(8,128)(2,1)}, f32[2,64,4096]{2,1,0:T(8,128)}, f32[2,64,4096]{2,1,0:T(8,128)}) fusion(bf16[2,512,4096]{2,1,0:T(8,128)(2,1)} %param.16, s32[]{:T(128)S(6)} %select_n.7, f32[]{:T(128)S(6)} %min_shard_map.3, bf16[2,64,4096]{2,1,0:T(8,128)(2,1)S(1)} %copy-done, f32[2,64,4096]{2,1,0:T(8,128)} %param.22, f32[2,64,4096]{2,1,0:T(8,128)} %param.19), kind=kLoop, calls=%fused_computation.29 | loop fusion | flops 8912896 | bytes 11534344 | tf_op jit(solution)/shard_map/convert_element_type | solution.py:11
  196.6 33.8 %all-gather.8.cloned.1.call-done = bf16[2,4096,512]{2,1,0:T(8,128)(2,1)} async-done(((bf16[2,512,512]{2,1,0:T(8,128)(2,1)}), bf16[2,4096,512]{2,1,0:T(8,128)(2,1)}) %all-gather.8.cloned.1.call-update) | async-done | bytes 8388624 | tf_op jit(solution)/shard_map/all_gather | solution.py:28
  230.5 47.7 %all-gather.4.cloned.1.call-done = bf16[2,512,4096]{2,1,0:T(8,128)(2,1)} async-done(((bf16[2,64,4096]{2,1,0:T(8,128)(2,1)}), bf16[2,512,4096]{2,1,0:T(8,128)(2,1)}) %all-gather.4.cloned.1.call-update) | async-done | bytes 8388624 | tf_op jit(solution)/shard_map/all_gather | solution.py:28
  278.1 47.7 %all-gather.6.cloned.1.call-done = bf16[2,512,4096]{2,1,0:T(8,128)(2,1)} async-done(((bf16[2,64,4096]{2,1,0:T(8,128)(2,1)}), bf16[2,512,4096]{2,1,0:T(8,128)(2,1)}) %all-gather.6.cloned.1.call-update) | async-done | bytes 8388624 | tf_op jit(solution)/shard_map/all_gather | solution.py:28
  325.8 7.9 %copy.24 = bf16[2,512,4096]{2,1,0:T(8,128)(2,1)} copy(bf16[2,512,4096]{2,1,0:T(8,128)(2,1)} %all-gather.4.cloned.1.call-done) | data formatting | bytes 16777216
  333.7 7.9 %copy.25 = bf16[2,512,4096]{2,1,0:T(8,128)(2,1)} copy(bf16[2,512,4096]{2,1,0:T(8,128)(2,1)} %all-gather.6.cloned.1.call-done) | data formatting | bytes 16777216
  341.6 7.3 %copy.26 = bf16[2,4096,512]{2,1,0:T(8,128)(2,1)} copy(bf16[2,4096,512]{2,1,0:T(8,128)(2,1)} %all-gather.8.cloned.1.call-done) | data formatting | bytes 16777216
  (8 shorter events, 0.2 us)
Async XLA Ops:
  7.2 54.0 %reduce-scatter.4.cloned.1.call-start = ((), (), s32[]{:S(2)}) async-start(), calls=%async_computation.3 | async-start | bytes 9437184 | tf_op jit(solution)/shard_map/reduce_scatter | solution.py:22
  8.0 103.7 %reduce-scatter.6.cloned.1.call-start = ((), (), s32[]{:S(2)}) async-start(), calls=%async_computation.4 | async-start | bytes 9437184 | tf_op jit(solution)/shard_map/reduce_scatter | solution.py:22
  8.8 153.3 %reduce-scatter.8.cloned.1.call-start = ((), (), s32[]{:S(2)}) async-start(), calls=%async_computation.5 | async-start | bytes 9437184 | tf_op jit(solution)/shard_map/reduce_scatter | solution.py:22
  9.6 220.9 %all-gather.8.cloned.1.call-start = ((), (), s32[]{:S(2)}) async-start(), calls=%async_computation.8 | async-start | bytes 9437184 | tf_op jit(solution)/shard_map/all_gather | solution.py:28
  179.2 6.1 %copy-start.1 = (bf16[2,64,4096]{2,1,0:T(8,128)(2,1)S(1)}, bf16[2,64,4096]{2,1,0:T(8,128)(2,1)}, u32[]{:S(2)}) copy-start(bf16[2,64,4096]{2,1,0:T(8,128)(2,1)} %reduce-scatter.4.cloned.1.call-done) | copy-start | bytes 3145732
  185.2 92.9 %all-gather.4.cloned.1.call-start = ((), (), s32[]{:S(2)}) async-start(), calls=%async_computation.6 | async-start | bytes 9437184 | tf_op jit(solution)/shard_map/all_gather | solution.py:28
  185.3 5.7 %copy-start = (bf16[2,64,4096]{2,1,0:T(8,128)(2,1)S(1)}, bf16[2,64,4096]{2,1,0:T(8,128)(2,1)}, u32[]{:S(2)}) copy-start(bf16[2,64,4096]{2,1,0:T(8,128)(2,1)} %reduce-scatter.6.cloned.1.call-done) | copy-start | bytes 3145732
  191.0 134.9 %all-gather.6.cloned.1.call-start = ((), (), s32[]{:S(2)}) async-start(), calls=%async_computation.7 | async-start | bytes 9437184 | tf_op jit(solution)/shard_map/all_gather | solution.py:28
Sparse Core Ops, SparseCore 0:
  10.3 50.8 reduce-scatter.3
  63.5 48.0 reduce-scatter.5
  113.9 48.0 reduce-scatter.7
  185.4 45.0 all-gather.7
  232.5 45.6 all-gather.3
  280.2 45.6 all-gather.5
where the time goes:
time: 356 us
  waiting for transfers between devices  278 us (78%)
  other arithmetic  24.2 us (7%)
  local copies, waits for them, and re-layouts  23.1 us (6%)
  between operations  16.8 us (5%)
  blocking collectives  13.4 us (4%)
    reduce_scatter x3, waiting for transfers between devices, step(): lax.psum_scatter(t[0], 'dp', scatter_dimension=1, tiled=True)  146 us
    all_gather x3, waiting for transfers between devices, step(): whole = [lax.all_gather(one[0], 'dp', axis=1, tiled=True) for one in new]  129 us
    unnamed x7, local copies, waits for them, and re-layouts  23.1 us
    convert_element_type x3, other arithmetic, adamw(): return ((w - 0.02 * step).astype(jnp.bfloat16), m, v)  17.1 us
    psum x1, blocking collectives, step(): squares = lax.psum(sum((jnp.sum(g * g) for g in gradients)), 'dp')  13.4 us
  transfers between devices with their start and end apart: 6, of which 6 were waited for; matrix products, arithmetic and copies ran while one was open for 4% of the time, Pallas kernels for 0%

commit v1 on v0

v1 whole, which is shorter than its diff:
```python
import functools

import jax
import jax.numpy as jnp
from jax import lax
from jax.experimental import pallas as pl
from jax.experimental.pallas import tpu as pltpu
from jax.sharding import PartitionSpec as P

MESH = pl.DeviceIdType.MESH
CORES = 2
PIECES = 4
TILE = (16, 512)
WAYS = (0, 1)
F32, BF16 = jnp.float32, jnp.bfloat16


def kernel(n, *refs):
    g, w, m_in, v_in, new, m, v = (refs[i : i + 3] for i in range(0, 21, 3))
    far, near, own_w = (refs[i : i + 3] for i in range(21, 30, 3))
    (acc, squares, term_sem, mate_sem, state_sem, far_sem, near_sem, ring_sem, ringfar_sem,
     back_sem, mate_send, back_send, sum_send, ring_send, square_send, square_sem) = refs[30:]

    chips = n // CORES
    me = lax.axis_index("dp")
    chip, core = me // CORES, me % CORES
    mate = chip * CORES + 1 - core
    right_chip, left_chip = lax.rem(chip + 1, chips), lax.rem(chip + chips - 1, chips)
    far_chip = lax.rem(chip + 2, chips)
    side = (right_chip * CORES + core, left_chip * CORES + core)
    arrays = range(3)
    layers = m[0].shape[0]
    half = layers // 2
    block_rows = [ref.shape[1] for ref in m]
    piece_rows = [r // PIECES for r in block_rows]
    steps = [(a, l) for l in range(half) for a in arrays]

    def rows(a, block, q):
        return pl.ds(pl.multiple_of(block * block_rows[a] + q * piece_rows[a], piece_rows[a]), piece_rows[a])

    def to(device):
        return {"device_id": {"dp": device}, "device_id_type": MESH}

    def mine(c):
        return c * CORES + core

    def mates(c):
        return c * CORES + 1 - core

    def tiles(a):
        columns = m[a].shape[2] // TILE[1]
        count = piece_rows[a] // TILE[0] * columns

        def at(i, base):
            r = pl.multiple_of(base + i // columns * TILE[0], TILE[0])
            c = pl.multiple_of(i % columns * TILE[1], TILE[1])
            return pl.ds(r, TILE[0]), pl.ds(c, TILE[1])

        return count, at

    targets = (far_chip, right_chip, left_chip, chip)
    places = [(t, a, layer) for t in range(4) for a in arrays for layer in range(layers)]

    def term(t, a, layer, q):
        where = rows(a, mine(targets[t]), q)
        return pltpu.make_async_copy(g[a].at[0, layer, where, :], new[a].at[layer, where, :], term_sem.at[t, a, layer, q])

    def mate_term(t, a, layer, q):
        theirs = new[a].at[layer, rows(a, mine(targets[t]), q), :]
        return pltpu.make_async_remote_copy(
            src_ref=g[a].at[0, layer, rows(a, mates(targets[t]), q), :], dst_ref=theirs,
            send_sem=mate_send.at[a], recv_sem=mate_sem.at[t, a, layer, q], **to(mate))

    def states(a):
        own = pl.ds(pl.multiple_of(me * block_rows[a], block_rows[a]), block_rows[a])
        return (pltpu.make_async_copy(m_in[a], m[a], state_sem.at[0, a]),
                pltpu.make_async_copy(v_in[a], v[a], state_sem.at[1, a]),
                pltpu.make_async_copy(w[a].at[:, own, :], own_w[a], state_sem.at[2, a]))

    barrier = pltpu.get_barrier_semaphore()
    for o in range(1, n):
        pl.semaphore_signal(barrier, inc=1, **to(lax.rem(me + o, n)))
    for t, a, layer in places[: 3 * layers]:
        @pl.loop(0, PIECES)
        def _(q):
            term(t, a, layer, q).start()
    pl.semaphore_wait(barrier, n - 1)

    order = [(t, a, layer) for t in range(4) for a, l in steps for layer in (l, half + l)]
    for t, a, layer in order:
        @pl.loop(0, PIECES)
        def _(q):
            mate_term(t, a, layer, q).start()
            if t > 0:
                term(t, a, layer, q).start()
    for a in arrays:
        for copy in states(a):
            copy.start()
    acc[...] = jnp.zeros_like(acc)

    def chip_sum(t, a, layer, q, more, write):
        term(t, a, layer, q).wait()
        mate_term(t, a, layer, q).wait_recv()
        count, at = tiles(a)
        first = mine(targets[t]) * block_rows[a] + q * piece_rows[a]
        second = mates(targets[t]) * block_rows[a] + q * piece_rows[a]

        def tile(i, carry):
            total = new[a][(layer, *at(i, first))].astype(F32) + new[a][(layer, *at(i, second))].astype(F32)
            for ref, index in more:
                total = total + ref[(*index, *at(i, q * piece_rows[a]))].astype(F32)
            return write(i, total, carry)

        return tile, count, at, first

    def summed(t, a, layer, q, more=()):
        def write(i, total, carry):
            new[a][(layer, *at(i, first))] = total.astype(BF16)
            return carry

        tile, count, at, first = chip_sum(t, a, layer, q, more, write)
        lax.fori_loop(0, count, lambda i, carry: tile(i, carry), 0)
        return new[a].at[layer, rows(a, mine(targets[t]), q), :]

    def local(a, q):
        return pl.ds(pl.multiple_of(q * piece_rows[a], piece_rows[a]), piece_rows[a])

    def to_far(way, a, l, q, src):
        return pltpu.make_async_remote_copy(
            src_ref=src, dst_ref=far[a].at[way, l, local(a, q), :],
            send_sem=sum_send.at[way, a], recv_sem=far_sem.at[way, a, l, q], **to(side[way]))

    def to_near(way, a, layer, q, src):
        return pltpu.make_async_remote_copy(
            src_ref=src, dst_ref=near[a].at[way, layer, local(a, q), :],
            send_sem=sum_send.at[way, a], recv_sem=near_sem.at[way, a, layer, q], **to(side[way]))

    for a, l in steps:
        @pl.loop(0, PIECES)
        def _(q):
            for way in WAYS:
                to_far(way, a, l, q, summed(0, a, way * half + l, q)).start()
    for a, l in steps:
        @pl.loop(0, PIECES)
        def _(q):
            for way in WAYS:
                layer = (1 - way) * half + l
                to_near(way, a, layer, q, summed(1 + way, a, layer, q)).start()
    for a, l in steps:
        @pl.loop(0, PIECES)
        def _(q):
            for way in WAYS:
                layer = way * half + l
                src = new[a].at[layer, rows(a, mine(targets[1 + way]), q), :]
                to_far(way, a, l, q, src).wait_recv()
                to_near(way, a, layer, q, summed(1 + way, a, layer, q, [(far[a], (way, l))])).start()
    for a, l in steps:
        @pl.loop(0, PIECES)
        def _(q):
            for layer in (l, half + l):
                for way in WAYS:
                    to_near(way, a, layer, q, near[a].at[way, layer, local(a, q), :]).wait_recv()

                def write(i, total, carry):
                    rounded = total.astype(BF16)
                    near[a][(0, layer, *at(i, q * piece_rows[a]))] = rounded
                    rounded = rounded.astype(F32)
                    square = rounded * rounded
                    for r in range(0, TILE[0], 8):
                        for c in range(0, TILE[1], 128):
                            carry = carry + square[r : r + 8, c : c + 128]
                    return carry

                tile, count, at, _ = chip_sum(3, a, layer, q, [(near[a], (way, layer)) for way in WAYS], write)
                acc[...] = lax.fori_loop(0, count, lambda i, carry: tile(i, carry), acc[...])

    def drain(sem, ref):
        pltpu.make_async_copy(ref, ref, sem).wait()

    squares[me] = acc[...]
    for way in WAYS:
        for a in arrays:
            drain(sum_send.at[way, a], new[a].at[:half, pl.ds(0, 3 * block_rows[a]), :])

    def square(o, device):
        return pltpu.make_async_remote_copy(
            src_ref=squares.at[device], dst_ref=squares.at[device],
            send_sem=square_send.at[o], recv_sem=square_sem.at[device], **to(lax.rem(me + o, n)))

    for o in range(1, n):
        square(o, me).start()
    for a in arrays:
        for copy in states(a):
            copy.wait()
    for o in range(1, n):
        square(o, lax.rem(me + o, n)).wait_recv()
    total = squares[0]
    for i in range(1, n):
        total = total + squares[i]
    total = jnp.sum(jnp.sum(total, axis=1, keepdims=True), axis=0, keepdims=True)
    count = n * sum(ref.size for ref in m)
    factor = jnp.minimum(1.0, 0.5 * lax.rsqrt(total / count + 1e-30))

    def ring(way, a, block, layer, q, sem):
        part = new[a].at[layer, rows(a, block, q), :]
        return pltpu.make_async_remote_copy(
            src_ref=part, dst_ref=part, send_sem=ring_send.at[way, a], recv_sem=sem, **to(side[way]))

    def back(a, block, layer, q):
        part = new[a].at[layer, rows(a, block, q), :]
        return pltpu.make_async_remote_copy(
            src_ref=part, dst_ref=part, send_sem=back_send.at[a], recv_sem=back_sem.at[a], **to(mate))

    for a, l in steps:
        @pl.loop(0, PIECES)
        def _(q):
            tile_count, at = tiles(a)
            for way in WAYS:
                layer = way * half + l

                def tile(i, carry):
                    here = (layer, *at(i, q * piece_rows[a]))
                    gradient = near[a][(0, *here)].astype(F32) * factor
                    mean = 0.9 * m[a][here] + 0.1 * gradient
                    variance = 0.95 * v[a][here] + 0.05 * gradient * gradient
                    weight = own_w[a][here].astype(F32)
                    step = mean * lax.rsqrt(variance + 1e-8) + 0.1 * weight
                    m[a][here] = mean
                    v[a][here] = variance
                    new[a][(layer, *at(i, me * block_rows[a] + q * piece_rows[a]))] = (weight - 0.02 * step).astype(BF16)
                    return carry

                lax.fori_loop(0, tile_count, tile, 0)
                ring(way, a, me, layer, q, ring_sem.at[way, a, layer, q]).start()
                back(a, me, layer, q).start()
    for a, l in steps:
        @pl.loop(0, PIECES)
        def _(q):
            for way in WAYS:
                layer = (1 - way) * half + l
                ring(way, a, me, layer, q, ring_sem.at[way, a, layer, q]).start()
    source = (mine(left_chip), mine(right_chip))
    for a, l in steps:
        @pl.loop(0, PIECES)
        def _(q):
            for way in WAYS:
                layer = way * half + l
                ring(way, a, source[way], layer, q, ring_sem.at[way, a, layer, q]).wait_recv()
                ring(way, a, source[way], layer, q, ringfar_sem.at[way, a, l, q]).start()
                back(a, source[way], layer, q).start()
    for a, l in steps:
        @pl.loop(0, PIECES)
        def _(q):
            for way in WAYS:
                layer = (1 - way) * half + l
                ring(way, a, source[way], layer, q, ring_sem.at[way, a, layer, q]).wait_recv()
                back(a, source[way], layer, q).start()
    for a, l in steps:
        @pl.loop(0, PIECES)
        def _(q):
            for way in WAYS:
                layer = way * half + l
                ring(way, a, mine(far_chip), layer, q, ringfar_sem.at[way, a, l, q]).wait_recv()
                back(a, mine(far_chip), layer, q).start()
    for a in arrays:
        whole = new[a].at[:half]
        drain(back_sem.at[a], whole)
        drain(back_send.at[a], whole)
        drain(mate_send.at[a], whole)
        for way in WAYS:
            drain(ring_send.at[way, a], new[a].at[:half, pl.ds(0, 3 * block_rows[a]), :])
    for o in range(1, n):
        square(o, me).wait_send()


def write_out(*refs):
    count = len(refs) // 2
    copies = [pltpu.make_async_copy(refs[i], refs[count + i], refs[-1].at[i]) for i in range(count)]
    for copy in copies:
        copy.start()
    for copy in copies:
        copy.wait()


def solution(mesh):
    n = mesh.shape["dp"]

    def step(*arrays):
        terms, weights, m, v = (arrays[i : i + 3] for i in (0, 3, 6, 9))
        layers = m[0].shape[0]
        hbm = pl.BlockSpec(memory_space=pltpu.HBM)
        dma = pltpu.SemaphoreType.DMA
        blocks = [one.shape[1:] for one in m]
        out = [(w.shape, BF16) for w in weights] + [(x.shape, F32) for x in (*m, *v)]
        scratch = (
            [pltpu.VMEM((2, layers // 2, *b), BF16) for b in blocks]
            + [pltpu.VMEM((2, layers, *b), BF16) for b in blocks]
            + [pltpu.VMEM((layers, *b), BF16) for b in blocks]
            + [pltpu.VMEM((8, 128), F32), pltpu.VMEM((n, 8, 128), F32)]
            + [dma((4, 3, layers, PIECES)), dma((4, 3, layers, PIECES)), dma((3, 3))]
            + [dma((2, 3, layers // 2, PIECES)), dma((2, 3, layers, PIECES))]
            + [dma((2, 3, layers, PIECES)), dma((2, 3, layers // 2, PIECES))]
            + [dma((3,)), dma((3,)), dma((3,)), dma((2, 3)), dma((2, 3)), dma((n,)), dma((n,))]
        )
        results = pl.pallas_call(
            functools.partial(kernel, n),
            out_shape=[pltpu.VMEM(shape, dtype) for shape, dtype in out],
            in_specs=[hbm] * len(arrays),
            out_specs=[pl.BlockSpec(memory_space=pltpu.VMEM)] * len(out),
            scratch_shapes=scratch,
            compiler_params=pltpu.CompilerParams(
                collective_id=0, has_side_effects=True, vmem_limit_bytes=16 * 2**20),
        )(*arrays)
        return pl.pallas_call(
            write_out,
            out_shape=[jax.ShapeDtypeStruct(shape, dtype) for shape, dtype in out],
            in_specs=[pl.BlockSpec(memory_space=pltpu.VMEM)] * len(out),
            out_specs=[hbm] * len(out),
            scratch_shapes=[dma((len(out),))],
            compiler_params=pltpu.CompilerParams(vmem_limit_bytes=2**20),
        )(*[pltpu.with_memory_space_constraint(x, pltpu.VMEM) for x in results])

    all_of, cut = P(None, None, None), P(None, "dp", None)
    return jax.shard_map(
        step,
        mesh=mesh,
        in_specs=(P(("rep", "dp"), None, None, None),) * 3 + (all_of,) * 3 + (cut,) * 6,
        out_specs=(P("rep", None, None),) * 3 + (P("rep", "dp", None),) * 6,
        check_vma=False,
    )
```

time: 356 us -> 264 us (0.74)
  waiting for transfers between devices: 278 us -> 0 us
  Pallas kernels: 0 us -> 235 us
  other arithmetic: 24.2 us -> 0 us
  between operations: 16.8 us -> 0.68 us
  blocking collectives: 13.4 us -> 0 us
  local copies, waits for them, and re-layouts: 23.1 us -> 28.1 us
    pallas_call x0 -> x2, Pallas kernels: none -> 235 us  [the longest x1 223 us: step(): pl.pallas_call(functools.partial(kernel, n), out_shape=[pltpu.VMEM(shape,...]
    reduce_scatter x3 -> x0, waiting for transfers between devices: 146 us -> none  [step(): lax.psum_scatter(t[0], 'dp', scatter_dimension=1, tiled=True)]
    all_gather x3 -> x0, waiting for transfers between devices: 129 us -> none  [step(): whole = [lax.all_gather(one[0], 'dp', axis=1, tiled=True) for one in new]]
    convert_element_type x3 -> x0, other arithmetic: 17.1 us -> none  [adamw(): return ((w - 0.02 * step).astype(jnp.bfloat16), m, v)]
    psum x1 -> x0, blocking collectives: 13.4 us -> none  [step(): squares = lax.psum(sum((jnp.sum(g * g) for g in gradients)), 'dp')]
    reduce_sum x3 -> x0, other arithmetic: 7.11 us -> none  [step(): squares = lax.psum(sum((jnp.sum(g * g) for g in gradients)), 'dp')]
    unnamed x7 -> x28, local copies, waits for them, and re-layouts: 23.1 us -> 28.1 us
  transfers between devices with their start and end apart: 6 -> 0, of which waited for: 6 -> 0; matrix products, arithmetic and copies ran while one was open for 4% -> 0% of each run, Pallas kernels for 0% -> 0%
where the time goes in v1:
time: 264 us
  Pallas kernels  235 us (89%)
  local copies, waits for them, and re-layouts  28.1 us (11%)
    pallas_call x1, Pallas kernels, step(): pl.pallas_call(functools.partial(kernel, n), out_shape=[pltpu.VMEM(shape,...  223 us
    unnamed x28, local copies, waits for them, and re-layouts  28.1 us
    pallas_call x1, Pallas kernels, step(): pl.pallas_call(write_out, out_shape=[jax.ShapeDtypeStruct(shape, dtype) f...  12.4 us

profile of v1, /device:TPU:113, one launch (start us, length us, event | category | flops | bytes accessed | tf_op | source)
XLA Modules:
  0.0 263.9 jit_solution(17653639190646138973)
XLA Ops:
  0.6 222.8 %shard_map.187 = (bf16[2,512,4096]{2,1,0:T(8,128)(2,1)S(1)}, bf16[2,512,4096]{2,1,0:T(8,128)(2,1)S(1)}, bf16[2,4096,512]{2,1,0:T(8,128)(2,1)S(1)}, f32[2,64,4096...) custom-call(bf16[1,2,512,4096]{3,2,1,0:T(8,128)(2,1)} %refs_0_.1, ...), custom_call_target="tpu_custom_call" | custom-call | tf_op jit(solution)/shard_map/pallas_call | solution.py:305
  223.4 0.0 copy-start
  223.4 3.4 %copy-done = bf16[2,512,4096]{2,1,0:T(8,128)(2,1)} copy-done((bf16[2,512,4096]{2,1,0:T(8,128)(2,1)}, bf16[2,512,4096]{2,1,0:T(8,128)(2,1)S(1)}, u32[]{:S(2)}) %copy-start) | copy-done | bytes 8388632
  226.8 0.0 copy-start.2
  226.8 3.4 %copy-done.2 = bf16[2,4096,512]{2,1,0:T(8,128)(2,1)} copy-done((bf16[2,4096,512]{2,1,0:T(8,128)(2,1)}, bf16[2,4096,512]{2,1,0:T(8,128)(2,1)S(1)}, u32[]{:S(2)}) %copy-start.2) | copy-done | bytes 8388632
  230.2 0.0 copy-start.4
  230.2 1.3 copy-done.4
  231.5 0.0 copy-start.6
  231.5 1.3 copy-done.6
  232.9 0.0 copy-start.8
  232.9 1.3 copy-done.8
  234.2 0.0 copy-start.10
  234.2 1.3 copy-done.10
  235.5 0.0 copy-start.12
  235.5 1.3 copy-done.12
  236.8 0.0 copy-start.1
  236.8 3.4 %copy-done.1 = bf16[2,512,4096]{2,1,0:T(8,128)(2,1)S(1)} copy-done((bf16[2,512,4096]{2,1,0:T(8,128)(2,1)S(1)}, bf16[2,512,4096]{2,1,0:T(8,128)(2,1)}, u32[]{:S(2)}) %copy-start.1) | copy-done | bytes 8388632
  240.2 3.4 %copy-done.3 = bf16[2,4096,512]{2,1,0:T(8,128)(2,1)S(1)} copy-done((bf16[2,4096,512]{2,1,0:T(8,128)(2,1)S(1)}, bf16[2,4096,512]{2,1,0:T(8,128)(2,1)}, u32[]{:S(2)}) %copy-start.3) | copy-done | bytes 8388632
  243.6 1.6 copy-done.5
  245.2 1.6 copy-done.7
  246.8 1.6 copy-done.9
  248.4 1.6 copy-done.11
  250.0 1.6 copy-done.13
  251.5 12.4 %shard_map.188 = (bf16[2,512,4096]{2,1,0:T(8,128)(2,1)}, bf16[2,512,4096]{2,1,0:T(8,128)(2,1)}, bf16[2,4096,512]{2,1,0:T(8,128)(2,1)}, f32[2,64,4096]{2,1,0:T(8,...) custom-call(bf16[2,512,4096]{2,1,0:T(8,128)(2,1)S(1)} %get-tuple-ele, ...), custom_call_target="tpu_custom_call" | custom-call | tf_op jit(solution)/shard_map/pallas_call | solution.py:314
  (6 shorter events, 0.0 us)
Async XLA Ops:
  223.4 3.4 %copy-start = (bf16[2,512,4096]{2,1,0:T(8,128)(2,1)}, bf16[2,512,4096]{2,1,0:T(8,128)(2,1)S(1)}, u32[]{:S(2)}) copy-start(bf16[2,512,4096]{2,1,0:T(8,128)(2,1)S(1)} %get-tuple-element.19.refs_1_) | copy-start | bytes 25165828
  226.8 3.4 %copy-start.2 = (bf16[2,4096,512]{2,1,0:T(8,128)(2,1)}, bf16[2,4096,512]{2,1,0:T(8,128)(2,1)S(1)}, u32[]{:S(2)}) copy-start(bf16[2,4096,512]{2,1,0:T(8,128)(2,1)S(1)} %get-tuple-element.20.refs_2_) | copy-start | bytes 25165828
  230.2 1.3 copy-start.4
  231.5 1.3 copy-start.6
  232.9 1.3 copy-start.8
  234.2 1.3 copy-start.10
  235.5 1.3 copy-start.12
  236.8 3.4 %copy-start.1 = (bf16[2,512,4096]{2,1,0:T(8,128)(2,1)S(1)}, bf16[2,512,4096]{2,1,0:T(8,128)(2,1)}, u32[]{:S(2)}) copy-start(bf16[2,512,4096]{2,1,0:T(8,128)(2,1)} %copy-done) | copy-start | bytes 25165828
  240.2 3.4 %copy-start.3 = (bf16[2,4096,512]{2,1,0:T(8,128)(2,1)S(1)}, bf16[2,4096,512]{2,1,0:T(8,128)(2,1)}, u32[]{:S(2)}) copy-start(bf16[2,4096,512]{2,1,0:T(8,128)(2,1)} %copy-done.2) | copy-start | bytes 25165828
  243.6 1.6 copy-start.5
  245.2 1.6 copy-start.7
  246.8 1.6 copy-start.9
  248.4 1.6 copy-start.11
  250.0 1.6 copy-start.13

commit v2 on v1

--- a/solution.py
+++ b/solution.py
@@ -317,7 +317,7 @@
             in_specs=[pl.BlockSpec(memory_space=pltpu.VMEM)] * len(out),
             out_specs=[hbm] * len(out),
             scratch_shapes=[dma((len(out),))],
-            compiler_params=pltpu.CompilerParams(vmem_limit_bytes=2**20),
+            compiler_params=pltpu.CompilerParams(vmem_limit_bytes=16 * 2**20),
         )(*[pltpu.with_memory_space_constraint(x, pltpu.VMEM) for x in results])
 
     all_of, cut = P(None, None, None), P(None, "dp", None)

time: 264 us -> 236 us (0.89)
  local copies, waits for them, and re-layouts: 28.1 us -> 0 us
    unnamed x28 -> x0, local copies, waits for them, and re-layouts: 28.1 us -> none
where the time goes in v2:
time: 236 us
  Pallas kernels  235 us (100%)
    pallas_call x1, Pallas kernels, step(): pl.pallas_call(functools.partial(kernel, n), out_shape=[pltpu.VMEM(shape,...  223 us
    pallas_call x1, Pallas kernels, step(): pl.pallas_call(write_out, out_shape=[jax.ShapeDtypeStruct(shape, dtype) f...  12.4 us

profile of v2, /device:TPU:113, one launch (start us, length us, event | category | flops | bytes accessed | tf_op | source)
XLA Modules:
  0.0 235.8 jit_solution(15792279577852697041)
XLA Ops:
  0.6 222.8 %shard_map.187 = (bf16[2,512,4096]{2,1,0:T(8,128)(2,1)S(1)}, bf16[2,512,4096]{2,1,0:T(8,128)(2,1)S(1)}, bf16[2,4096,512]{2,1,0:T(8,128)(2,1)S(1)}, f32[2,64,4096...) custom-call(bf16[1,2,512,4096]{3,2,1,0:T(8,128)(2,1)} %refs_0_.1, ...), custom_call_target="tpu_custom_call" | custom-call | tf_op jit(solution)/shard_map/pallas_call | solution.py:305
  223.4 12.4 %shard_map.188 = (bf16[2,512,4096]{2,1,0:T(8,128)(2,1)}, bf16[2,512,4096]{2,1,0:T(8,128)(2,1)}, bf16[2,4096,512]{2,1,0:T(8,128)(2,1)}, f32[2,64,4096]{2,1,0:T(8,...) custom-call(bf16[2,512,4096]{2,1,0:T(8,128)(2,1)S(1)} %get-tuple-ele, ...), custom_call_target="tpu_custom_call" | custom-call | tf_op jit(solution)/shard_map/pallas_call | solution.py:314

commit v3 on v0

v3 whole, which is shorter than its diff:
```python
import functools

import jax
import jax.numpy as jnp
from jax import lax
from jax.experimental import pallas as pl
from jax.experimental.pallas import tpu as pltpu
from jax.sharding import PartitionSpec as P

MESH = pl.DeviceIdType.MESH
CORES = 2
PIECES = 8
TILE = (16, 512)
WAYS = (0, 1)
F32, BF16 = jnp.float32, jnp.bfloat16


def kernel(n, fine, *refs):
    g, w, m_in, v_in, new, m, v = (refs[i : i + 3] for i in range(0, 21, 3))
    far, near, own_w = (refs[i : i + 3] for i in range(21, 30, 3))
    (stage, acc, squares, term_sem, mate_sem, head_sem, stage_sem, state_sem, first_sem, second_sem, last_sem,
     back_sem, mate_send, back_send, sum_send, ring_send, square_sem) = refs[30:]

    chips = n // CORES
    me = lax.axis_index("dp")
    chip, core = me // CORES, me % CORES
    mate = chip * CORES + 1 - core
    right_chip, left_chip = lax.rem(chip + 1, chips), lax.rem(chip + chips - 1, chips)
    far_chip = lax.rem(chip + 2, chips)
    side = (right_chip * CORES + core, left_chip * CORES + core)
    layers = m[0].shape[0]
    half = layers // 2
    height = [ref.shape[1] for ref in m]
    arrays = [a for a in range(3) if a != fine] + [fine]
    steps = [(k, a, l) for k, (l, a) in enumerate((l, a) for l in range(half) for a in arrays)]
    final = len(steps) - 1
    head_first = steps[final:] + steps[:final]

    def to(device):
        return {"device_id": {"dp": device}, "device_id_type": MESH}

    def mine(c):
        return c * CORES + core

    def mates(c):
        return c * CORES + 1 - core

    def block(a, index, start=0, size=None):
        size = size or height[a]
        return pl.ds(pl.multiple_of(index * height[a] + start, size), size)

    def pieces(k, a, body):
        if k < final:
            body(0, 0, height[a])
        else:
            size = height[a] // PIECES
            pl.loop(0, PIECES)(lambda q: body(q, q * size, size))

    def tiles(a, size, body, carry):
        columns = m[a].shape[2] // TILE[1]

        def tile(i, carry):
            def at(base):
                r = pl.multiple_of(base + i // columns * TILE[0], TILE[0])
                return pl.ds(r, TILE[0]), pl.ds(pl.multiple_of(i % columns * TILE[1], TILE[1]), TILE[1])

            return body(at, carry)

        return lax.fori_loop(0, size // TILE[0] * columns, tile, carry)

    def drain(sem, ref):
        pltpu.make_async_copy(ref, ref, sem).wait()

    targets = (far_chip, right_chip, left_chip, chip)

    def term(t, a):
        where = block(a, mine(targets[t]))
        return pltpu.make_async_copy(g[a].at[0, :, where, :], new[a].at[:, where, :], term_sem.at[t, a])

    def mate_term(t, a):
        return pltpu.make_async_remote_copy(
            src_ref=g[a].at[0, :, block(a, mates(targets[t])), :], dst_ref=new[a].at[:, block(a, mine(targets[t])), :],
            send_sem=mate_send.at[a], recv_sem=mate_sem.at[t, a], **to(mate))

    def mate_head(q):
        size = height[fine] // PIECES
        return pltpu.make_async_remote_copy(
            src_ref=stage.at[:, block(fine, 0, q * size, size), :],
            dst_ref=new[fine].at[:, block(fine, mine(far_chip), q * size, size), :],
            send_sem=mate_send.at[fine], recv_sem=head_sem.at[q], **to(mate))

    to_stage = pltpu.make_async_copy(g[fine].at[0, :, block(fine, mates(far_chip)), :], stage, stage_sem.at[0])

    def states(a):
        return (pltpu.make_async_copy(m_in[a], m[a], state_sem.at[0, a]),
                pltpu.make_async_copy(v_in[a], v[a], state_sem.at[1, a]),
                pltpu.make_async_copy(w[a].at[:, block(a, me), :], own_w[a], state_sem.at[2, a]))

    barrier = pltpu.get_barrier_semaphore()
    for o in range(1, n):
        pl.semaphore_signal(barrier, inc=1, **to(lax.rem(me + o, n)))
    to_stage.start()
    for a in (fine, *arrays[:-1]):
        term(0, a).start()
    to_stage.wait()
    pl.semaphore_wait(barrier, n - 1)
    pl.loop(0, PIECES)(lambda q: mate_head(q).start())
    for t, a in [(0, a) for a in arrays[:-1]] + [(t, a) for a in arrays for t in (1, 2)] + [(3, a) for a in arrays]:
        mate_term(t, a).start()
        if t > 0:
            term(t, a).start()
    for a in arrays:
        for copy in states(a):
            copy.start()
    acc[...] = jnp.zeros_like(acc)

    arrived = set()

    def await_terms(t, a):
        if (t, a) not in arrived:
            arrived.add((t, a))
            term(t, a).wait()
            if (t, a) == (0, fine):
                return lambda q: mate_head(q).wait_recv()
            mate_term(t, a).wait_recv()
        return lambda q: None

    def total(t, a, layer, at, start, more):
        out = new[a][(layer, *at(mine(targets[t]) * height[a] + start))].astype(F32)
        out = out + new[a][(layer, *at(mates(targets[t]) * height[a] + start))].astype(F32)
        for ref, index in more:
            out = out + ref[(*index, *at(start))].astype(F32)
        return out

    def summed(t, a, layer, start, size, more=()):
        def tile(at, carry):
            new[a][(layer, *at(mine(targets[t]) * height[a] + start))] = total(t, a, layer, at, start, more).astype(BF16)
            return carry

        tiles(a, size, tile, 0)
        return new[a].at[layer, block(a, mine(targets[t]), start, size), :]

    def send_sum(way, a, src, dst, sem):
        pltpu.make_async_remote_copy(
            src_ref=src, dst_ref=dst, send_sem=sum_send.at[way, a], recv_sem=sem, **to(side[way])).start()

    def part(a, start, size):
        return pl.ds(pl.multiple_of(start, size), size)

    for k, a, l in head_first:
        here = await_terms(0, a)

        def body(q, start, size):
            here(q)
            for way in WAYS:
                src = summed(0, a, way * half + l, start, size)
                send_sum(way, a, src, far[a].at[way, l, part(a, start, size), :], first_sem.at[way, k])

        pieces(k, a, body)
    for k, a, l in steps:
        for way in WAYS:
            await_terms(1 + way, a)
            layer = (1 - way) * half + l
            src = summed(1 + way, a, layer, 0, height[a])
            send_sum(way, a, src, near[a].at[way, layer], second_sem.at[way, k])
    for k, a, l in steps:
        for way in WAYS:
            drain(first_sem.at[way, k], far[a].at[way, l])

        def body(q, start, size):
            for way in WAYS:
                layer = way * half + l
                src = summed(1 + way, a, layer, start, size, [(far[a], (way, l))])
                send_sum(way, a, src, near[a].at[way, layer, part(a, start, size), :], last_sem.at[way, k + q])

        pieces(k, a, body)
    for k, a, l in steps:
        await_terms(3, a)
        for way in WAYS:
            drain(second_sem.at[way, k], near[a].at[way, (1 - way) * half + l])

        def body(q, start, size):
            for way in WAYS:
                layer = way * half + l
                drain(last_sem.at[way, k + q], near[a].at[way, layer, part(a, start, size), :])

                def tile(at, carry):
                    rounded = total(3, a, layer, at, start, [(near[a], (i, layer)) for i in WAYS]).astype(BF16)
                    near[a][(0, layer, *at(start))] = rounded
                    rounded = rounded.astype(F32)
                    square = rounded * rounded
                    for r in range(0, TILE[0], 8):
                        for c in range(0, TILE[1], 128):
                            carry = carry + square[r : r + 8, c : c + 128]
                    return carry

                acc[...] = tiles(a, size, tile, acc[...])

        pieces(k, a, body)

    squares[me] = acc[...]
    for way in WAYS:
        for a in arrays:
            drain(sum_send.at[way, a], new[a].at[:half, pl.ds(0, 3 * height[a]), :])
    for o in range(1, n):
        pltpu.make_async_remote_copy(
            src_ref=squares.at[me], dst_ref=squares.at[me], send_sem=square_sem.at[0], recv_sem=square_sem.at[1],
            **to(lax.rem(me + o, n))).start()
    for a in arrays:
        for copy in states(a):
            copy.wait()
    drain(square_sem.at[1], squares.at[pl.ds(0, n - 1)])
    everyone = squares[0]
    for i in range(1, n):
        everyone = everyone + squares[i]
    everyone = jnp.sum(jnp.sum(everyone, axis=1, keepdims=True), axis=0, keepdims=True)
    count = n * sum(ref.size for ref in m)
    factor = jnp.minimum(1.0, 0.5 * lax.rsqrt(everyone / count + 1e-30))

    def ring(way, a, index, layer, start, size, sem):
        here = new[a].at[layer, block(a, index, start, size), :]
        pltpu.make_async_remote_copy(
            src_ref=here, dst_ref=here, send_sem=ring_send.at[way, a], recv_sem=sem, **to(side[way])).start()

    def back(a, index, layer, start, size):
        here = new[a].at[layer, block(a, index, start, size), :]
        pltpu.make_async_remote_copy(
            src_ref=here, dst_ref=here, send_sem=back_send.at[a], recv_sem=back_sem.at[a], **to(mate)).start()

    for k, a, l in head_first:
        def body(q, start, size):
            for way in WAYS:
                layer = way * half + l

                def tile(at, carry):
                    here = (layer, *at(start))
                    gradient = near[a][(0, *here)].astype(F32) * factor
                    mean = 0.9 * m[a][here] + 0.1 * gradient
                    variance = 0.95 * v[a][here] + 0.05 * gradient * gradient
                    weight = own_w[a][here].astype(F32)
                    step = mean * lax.rsqrt(variance + 1e-8) + 0.1 * weight
                    m[a][here] = mean
                    v[a][here] = variance
                    new[a][(layer, *at(me * height[a] + start))] = (weight - 0.02 * step).astype(BF16)
                    return carry

                tiles(a, size, tile, 0)
                ring(way, a, me, layer, start, size, first_sem.at[way, k])
                back(a, me, layer, start, size)

        pieces(k, a, body)
    for k, a, l in steps:
        for way in WAYS:
            ring(way, a, me, (1 - way) * half + l, 0, height[a], second_sem.at[way, k])
    source = (mine(left_chip), mine(right_chip))
    for k, a, l in head_first:
        for way in WAYS:
            layer = way * half + l
            drain(first_sem.at[way, k], new[a].at[layer, block(a, source[way]), :])
            back(a, source[way], layer, 0, height[a])
    for k, a, l in steps:
        def body(q, start, size):
            for way in WAYS:
                ring(way, a, source[way], way * half + l, start, size, last_sem.at[way, k + q])

        pieces(k, a, body)
    for k, a, l in steps:
        for way in WAYS:
            layer = (1 - way) * half + l
            drain(second_sem.at[way, k], new[a].at[layer, block(a, source[way]), :])
            back(a, source[way], layer, 0, height[a])
    for k, a, l in steps:
        def body(q, start, size):
            for way in WAYS:
                layer = way * half + l
                drain(last_sem.at[way, k + q], new[a].at[layer, block(a, mine(far_chip), start, size), :])
                back(a, mine(far_chip), layer, start, size)

        pieces(k, a, body)
    for a in arrays:
        for sem in (mate_send, back_send, back_sem):
            drain(sem.at[a], new[a].at[:half])
        for way in WAYS:
            drain(ring_send.at[way, a], new[a].at[:half, pl.ds(0, 3 * height[a]), :])
    drain(square_sem.at[0], squares.at[pl.ds(0, n - 1)])


def write_out(*refs):
    count = len(refs) // 2
    copies = [pltpu.make_async_copy(refs[i], refs[count + i], refs[-1].at[i]) for i in range(count)]
    for copy in copies:
        copy.start()
    for copy in copies:
        copy.wait()


def solution(mesh):
    n = mesh.shape["dp"]

    def step(*arrays):
        terms, weights, m, v = (arrays[i : i + 3] for i in (0, 3, 6, 9))
        layers = m[0].shape[0]
        hbm = pl.BlockSpec(memory_space=pltpu.HBM)
        dma = pltpu.SemaphoreType.DMA
        blocks = [one.shape[1:] for one in m]
        out = [(w.shape, BF16) for w in weights] + [(x.shape, F32) for x in (*m, *v)]
        fine = max(range(3), key=lambda a: blocks[a][0])
        steps = 3 * (layers // 2)
        scratch = (
            [pltpu.VMEM((2, layers // 2, *b), BF16) for b in blocks]
            + [pltpu.VMEM((2, layers, *b), BF16) for b in blocks]
            + [pltpu.VMEM((layers, *b), BF16) for b in blocks]
            + [pltpu.VMEM((layers, *blocks[fine]), BF16), pltpu.VMEM((8, 128), F32), pltpu.VMEM((n, 8, 128), F32)]
            + [dma((4, 3)), dma((4, 3)), dma((PIECES,)), dma((1,)), dma((3, 3))]
            + [dma((2, steps)), dma((2, steps)), dma((2, steps - 1 + PIECES))]
            + [dma((3,)), dma((3,)), dma((3,)), dma((2, 3)), dma((2, 3)), dma((2,))]
        )
        results = pl.pallas_call(
            functools.partial(kernel, n, fine),
            out_shape=[pltpu.VMEM(shape, dtype) for shape, dtype in out],
            in_specs=[hbm] * len(arrays),
            out_specs=[pl.BlockSpec(memory_space=pltpu.VMEM)] * len(out),
            scratch_shapes=scratch,
            compiler_params=pltpu.CompilerParams(
                collective_id=0, has_side_effects=True, vmem_limit_bytes=16 * 2**20),
        )(*arrays)
        return pl.pallas_call(
            write_out,
            out_shape=[jax.ShapeDtypeStruct(shape, dtype) for shape, dtype in out],
            in_specs=[pl.BlockSpec(memory_space=pltpu.VMEM)] * len(out),
            out_specs=[hbm] * len(out),
            scratch_shapes=[dma((len(out),))],
            compiler_params=pltpu.CompilerParams(vmem_limit_bytes=16 * 2**20),
        )(*[pltpu.with_memory_space_constraint(x, pltpu.VMEM) for x in results])

    all_of, cut = P(None, None, None), P(None, "dp", None)
    return jax.shard_map(
        step,
        mesh=mesh,
        in_specs=(P(("rep", "dp"), None, None, None),) * 3 + (all_of,) * 3 + (cut,) * 6,
        out_specs=(P("rep", None, None),) * 3 + (P("rep", "dp", None),) * 6,
        check_vma=False,
    )
```

time: 356 us -> 232 us (0.65)
  waiting for transfers between devices: 278 us -> 0 us
  Pallas kernels: 0 us -> 231 us
  other arithmetic: 24.2 us -> 0 us
  local copies, waits for them, and re-layouts: 23.1 us -> 0 us
  between operations: 16.8 us -> 0.65 us
  blocking collectives: 13.4 us -> 0 us
    pallas_call x0 -> x2, Pallas kernels: none -> 231 us  [the longest x1 219 us: step(): pl.pallas_call(functools.partial(kernel, n, fine), out_shape=[pltpu.VMEM(...]
    reduce_scatter x3 -> x0, waiting for transfers between devices: 146 us -> none  [step(): lax.psum_scatter(t[0], 'dp', scatter_dimension=1, tiled=True)]
    all_gather x3 -> x0, waiting for transfers between devices: 129 us -> none  [step(): whole = [lax.all_gather(one[0], 'dp', axis=1, tiled=True) for one in new]]
    unnamed x7 -> x0, local copies, waits for them, and re-layouts: 23.1 us -> none
    convert_element_type x3 -> x0, other arithmetic: 17.1 us -> none  [adamw(): return ((w - 0.02 * step).astype(jnp.bfloat16), m, v)]
    psum x1 -> x0, blocking collectives: 13.4 us -> none  [step(): squares = lax.psum(sum((jnp.sum(g * g) for g in gradients)), 'dp')]
    reduce_sum x3 -> x0, other arithmetic: 7.11 us -> none  [step(): squares = lax.psum(sum((jnp.sum(g * g) for g in gradients)), 'dp')]
  transfers between devices with their start and end apart: 6 -> 0, of which waited for: 6 -> 0; matrix products, arithmetic and copies ran while one was open for 4% -> 0% of each run, Pallas kernels for 0% -> 0%
where the time goes in v3:
time: 232 us
  Pallas kernels  231 us (100%)
    pallas_call x1, Pallas kernels, step(): pl.pallas_call(functools.partial(kernel, n, fine), out_shape=[pltpu.VMEM(...  219 us
    pallas_call x1, Pallas kernels, step(): pl.pallas_call(write_out, out_shape=[jax.ShapeDtypeStruct(shape, dtype) f...  12.4 us

profile of v3, /device:TPU:113, one launch (start us, length us, event | category | flops | bytes accessed | tf_op | source)
XLA Modules:
  0.0 231.9 jit_solution(2647604874021261721)
XLA Ops:
  0.6 218.9 %shard_map.187 = (bf16[2,512,4096]{2,1,0:T(8,128)(2,1)S(1)}, bf16[2,512,4096]{2,1,0:T(8,128)(2,1)S(1)}, bf16[2,4096,512]{2,1,0:T(8,128)(2,1)S(1)}, f32[2,64,4096...) custom-call(bf16[1,2,512,4096]{3,2,1,0:T(8,128)(2,1)} %refs_0_.1, ...), custom_call_target="tpu_custom_call" | custom-call | tf_op jit(solution)/shard_map/pallas_call | solution.py:318
  219.5 12.4 %shard_map.188 = (bf16[2,512,4096]{2,1,0:T(8,128)(2,1)}, bf16[2,512,4096]{2,1,0:T(8,128)(2,1)}, bf16[2,4096,512]{2,1,0:T(8,128)(2,1)}, f32[2,64,4096]{2,1,0:T(8,...) custom-call(bf16[2,512,4096]{2,1,0:T(8,128)(2,1)S(1)} %get-tuple-ele, ...), custom_call_target="tpu_custom_call" | custom-call | tf_op jit(solution)/shard_map/pallas_call | solution.py:327

commit v4 on v3

--- a/solution.py
+++ b/solution.py
@@ -10,16 +10,19 @@
 MESH = pl.DeviceIdType.MESH
 CORES = 2
 PIECES = 8
+LAST_PIECES = 4
 TILE = (16, 512)
 WAYS = (0, 1)
 F32, BF16 = jnp.float32, jnp.bfloat16
+VMEM_LIMIT = 16 * 2**20
 
 
 def kernel(n, fine, *refs):
     g, w, m_in, v_in, new, m, v = (refs[i : i + 3] for i in range(0, 21, 3))
-    far, near, own_w = (refs[i : i + 3] for i in range(21, 30, 3))
+    tail, *refs = refs[21:]
+    far, near, own_w = (refs[i : i + 3] for i in range(0, 9, 3))
     (stage, acc, squares, term_sem, mate_sem, head_sem, stage_sem, state_sem, first_sem, second_sem, last_sem,
-     back_sem, mate_send, back_send, sum_send, ring_send, square_sem) = refs[30:]
+     back_sem, mate_send, back_send, sum_send, ring_send, square_sem, tail_sem) = refs[9:]
 
     chips = n // CORES
     me = lax.axis_index("dp")
@@ -257,55 +260,75 @@
         for way in WAYS:
             layer = way * half + l
             drain(first_sem.at[way, k], new[a].at[layer, block(a, source[way]), :])
-            back(a, source[way], layer, 0, height[a])
-    for k, a, l in steps:
+            if k < final:
+                back(a, source[way], layer, 0, height[a])
+            else:
+                here = new[a].at[layer, block(a, source[way]), :]
+                pltpu.make_async_remote_copy(
+                    src_ref=here, dst_ref=here, send_sem=tail_sem.at[2], recv_sem=tail_sem.at[way], **to(mate)).start()
+
+    def last_pieces(k, a, body):
+        if k < final - 1:
+            body(0, 0, height[a])
+        else:
+            size = height[a] // LAST_PIECES
+            pl.loop(0, LAST_PIECES)(lambda q: body(q, q * size, size))
+
+    for k, a, l in steps[:final]:
         def body(q, start, size):
             for way in WAYS:
                 ring(way, a, source[way], way * half + l, start, size, last_sem.at[way, k + q])
 
-        pieces(k, a, body)
+        last_pieces(k, a, body)
     for k, a, l in steps:
         for way in WAYS:
             layer = (1 - way) * half + l
             drain(second_sem.at[way, k], new[a].at[layer, block(a, source[way]), :])
             back(a, source[way], layer, 0, height[a])
-    for k, a, l in steps:
+    _, a, l = steps[final]
+    for way in WAYS:
+        drain(tail_sem.at[way], new[a].at[way * half + l, block(a, mates((left_chip, right_chip)[way])), :])
+    pair = CORES * height[a]
+    where = pl.ds(pl.multiple_of((left_chip + core * (right_chip - left_chip)) * pair, pair), pair)
+    to_tail = pltpu.make_async_copy(new[a].at[core * half + l, where, :], tail, tail_sem.at[3])
+    to_tail.start()
+    for k, a, l in steps[:final]:
         def body(q, start, size):
             for way in WAYS:
                 layer = way * half + l
                 drain(last_sem.at[way, k + q], new[a].at[layer, block(a, mine(far_chip), start, size), :])
                 back(a, mine(far_chip), layer, start, size)
 
-        pieces(k, a, body)
+        last_pieces(k, a, body)
+    to_tail.wait()
+    drain(tail_sem.at[2], new[fine].at[0, pl.ds(0, 2 * height[fine]), :])
     for a in arrays:
-        for sem in (mate_send, back_send, back_sem):
-            drain(sem.at[a], new[a].at[:half])
-        for way in WAYS:
-            drain(ring_send.at[way, a], new[a].at[:half, pl.ds(0, 3 * height[a]), :])
+        drain(mate_send.at[a], new[a].at[:half])
+        for sem in (back_send, back_sem):
+            drain(sem.at[a], new[a].at[:half] if a != fine else new[a].at[: layers - 1, pl.ds(0, 4 * height[a]), :])
+        for way in WAYS:
+            blocks = 3 * half - (a == fine)
+            drain(ring_send.at[way, a], new[a].at[0, pl.ds(0, blocks * height[a]), :])
     drain(square_sem.at[0], squares.at[pl.ds(0, n - 1)])
-
-
-def write_out(*refs):
-    count = len(refs) // 2
-    copies = [pltpu.make_async_copy(refs[i], refs[count + i], refs[-1].at[i]) for i in range(count)]
-    for copy in copies:
-        copy.start()
-    for copy in copies:
-        copy.wait()
 
 
 def solution(mesh):
     n = mesh.shape["dp"]
+    chips = n // CORES
+    onward = [(i, (i // CORES + (1 if i % CORES == 0 else chips - 1)) % chips * CORES + i % CORES) for i in range(n)]
+    mates = [(i, i // CORES * CORES + 1 - i % CORES) for i in range(n)]
 
     def step(*arrays):
         terms, weights, m, v = (arrays[i : i + 3] for i in (0, 3, 6, 9))
         layers = m[0].shape[0]
         hbm = pl.BlockSpec(memory_space=pltpu.HBM)
+        vmem = pl.BlockSpec(memory_space=pltpu.VMEM)
         dma = pltpu.SemaphoreType.DMA
         blocks = [one.shape[1:] for one in m]
+        fine = max(range(3), key=lambda a: blocks[a][0])
         out = [(w.shape, BF16) for w in weights] + [(x.shape, F32) for x in (*m, *v)]
-        fine = max(range(3), key=lambda a: blocks[a][0])
         steps = 3 * (layers // 2)
+        rows, columns = blocks[fine]
         scratch = (
             [pltpu.VMEM((2, layers // 2, *b), BF16) for b in blocks]
             + [pltpu.VMEM((2, layers, *b), BF16) for b in blocks]
@@ -313,25 +336,69 @@
             + [pltpu.VMEM((layers, *blocks[fine]), BF16), pltpu.VMEM((8, 128), F32), pltpu.VMEM((n, 8, 128), F32)]
             + [dma((4, 3)), dma((4, 3)), dma((PIECES,)), dma((1,)), dma((3, 3))]
             + [dma((2, steps)), dma((2, steps)), dma((2, steps - 1 + PIECES))]
-            + [dma((3,)), dma((3,)), dma((3,)), dma((2, 3)), dma((2, 3)), dma((2,))]
+            + [dma((3,)), dma((3,)), dma((3,)), dma((2, 3)), dma((2, 3)), dma((2,)), dma((4,))]
         )
-        results = pl.pallas_call(
+        *results, tail = pl.pallas_call(
             functools.partial(kernel, n, fine),
-            out_shape=[pltpu.VMEM(shape, dtype) for shape, dtype in out],
+            out_shape=[pltpu.VMEM(shape, dtype) for shape, dtype in [*out, ((CORES * rows, columns), BF16)]],
             in_specs=[hbm] * len(arrays),
-            out_specs=[pl.BlockSpec(memory_space=pltpu.VMEM)] * len(out),
+            out_specs=[vmem] * (len(out) + 1),
             scratch_shapes=scratch,
             compiler_params=pltpu.CompilerParams(
-                collective_id=0, has_side_effects=True, vmem_limit_bytes=16 * 2**20),
+                collective_id=0, has_side_effects=True, vmem_limit_bytes=VMEM_LIMIT),
         )(*arrays)
-        return pl.pallas_call(
-            write_out,
-            out_shape=[jax.ShapeDtypeStruct(shape, dtype) for shape, dtype in out],
-            in_specs=[pl.BlockSpec(memory_space=pltpu.VMEM)] * len(out),
-            out_specs=[hbm] * len(out),
-            scratch_shapes=[dma((len(out),))],
-            compiler_params=pltpu.CompilerParams(vmem_limit_bytes=16 * 2**20),
-        )(*[pltpu.with_memory_space_constraint(x, pltpu.VMEM) for x in results])
+
+        def held(x):
+            return pltpu.with_memory_space_constraint(x, pltpu.VMEM)
+
+        def write(indices, place=None, part=None, whole=None):
+            sources = [held(results[i]) for i in indices]
+            shapes = [jax.ShapeDtypeStruct(*out[i]) for i in indices]
+            specs, aliases = [vmem] * len(indices), {}
+            if part is not None:
+                aliases = {len(sources): len(shapes)}
+                sources += [whole, held(part)]
+                shapes.append(jax.ShapeDtypeStruct(*out[fine]))
+                specs = specs + [hbm, vmem]
+
+            def body(*refs):
+                ins, outs, sem = refs[: len(sources)], refs[len(sources) : -1], refs[-1]
+                copies = [pltpu.make_async_copy(ins[i], outs[i], sem.at[i]) for i in range(len(indices))]
+                if part is not None:
+                    layer, first = place(lax.axis_index("dp"))
+                    to = outs[-1].at[layer, pl.ds(pl.multiple_of(first, CORES * rows), CORES * rows), :]
+                    copies.append(pltpu.make_async_copy(ins[-1], to, sem.at[len(indices)]))
+                for copy in copies:
+                    copy.start()
+                for copy in copies:
+                    copy.wait()
+
+            moved = sum(x.size * x.dtype.itemsize for x in (*(results[i] for i in indices), *(() if part is None else (part,))))
+            return pl.pallas_call(
+                body,
+                out_shape=shapes,
+                in_specs=specs,
+                out_specs=[hbm] * len(shapes),
+                scratch_shapes=[dma((len(shapes),))],
+                input_output_aliases=aliases,
+                compiler_params=pltpu.CompilerParams(vmem_limit_bytes=VMEM_LIMIT),
+                cost_estimate=pl.CostEstimate(flops=0, bytes_accessed=2 * moved, transcendentals=0),
+            )(*sources)
+
+        def place_of(me, core):
+            far_chip = lax.rem(me // CORES + chips // 2, chips)
+            return core * (layers // 2) + layers // 2 - 1, far_chip * CORES * rows
+
+        own = lax.ppermute(tail, "dp", onward)
+        first = list(range(6))
+        done = dict(zip(first, write(first), strict=True))
+        own, done[fine] = lax.optimization_barrier((own, done[fine]))
+        mates_part = lax.ppermute(own, "dp", mates)
+        later = list(range(6, 9))
+        *got, whole = write(later, lambda me: place_of(me, lax.rem(me, CORES)), own, done[fine])
+        done.update(zip(later, got, strict=True))
+        (done[fine],) = write([], lambda me: place_of(me, 1 - lax.rem(me, CORES)), mates_part, whole)
+        return tuple(done[i] for i in range(9))
 
     all_of, cut = P(None, None, None), P(None, "dp", None)
     return jax.shard_map(

time: 232 us -> 229 us (0.987)
  Pallas kernels: 231 us -> 222 us
  starting transfers between devices: 0 us -> 3.56 us
    pallas_call x1, Pallas kernels: 219 us -> 208 us  [step(): pl.pallas_call(functools.partial(kernel, n, fine), out_shape=[pltpu.VMEM(...]
    ppermute x0 -> x2, starting transfers between devices: none -> 3.56 us  [the longest x1 2.2 us: step(): mates_part = lax.ppermute(own, 'dp', mates)]
    pallas_call x1 -> x3, Pallas kernels: 12.4 us -> 14.4 us  [write(): pl.pallas_call(body, out_shape=shapes, in_specs=specs, out_specs=[hbm] *...]
  transfers between devices with their start and end apart: 0 -> 2, of which waited for: 0 -> 1; matrix products, arithmetic and copies ran while one was open for 0% -> 0% of each run, Pallas kernels for 0% -> 6%
where the time goes in v4:
time: 229 us
  Pallas kernels  222 us (97%)
  starting transfers between devices  3.56 us (2%)
    pallas_call x1, Pallas kernels, step(): pl.pallas_call(functools.partial(kernel, n, fine), out_shape=[pltpu.VMEM(...  208 us
    pallas_call x3, Pallas kernels, write(): pl.pallas_call(body, out_shape=shapes, in_specs=specs, out_specs=[hbm] *...  14.4 us
  transfers between devices with their start and end apart: 2, of which 1 were waited for; matrix products, arithmetic and copies ran while one was open for 0% of the time, Pallas kernels for 6%

profile of v4, /device:TPU:113, one launch (start us, length us, event | category | flops | bytes accessed | tf_op | source)
XLA Modules:
  0.0 228.8 jit_solution(11919353514715411411)
XLA Ops:
  0.6 207.9 %shard_map.187 = (bf16[2,512,4096]{2,1,0:T(8,128)(2,1)S(1)}, bf16[2,512,4096]{2,1,0:T(8,128)(2,1)S(1)}, bf16[2,4096,512]{2,1,0:T(8,128)(2,1)S(1)}, f32[2,64,4096...) custom-call(bf16[1,2,512,4096]{3,2,1,0:T(8,128)(2,1)} %refs_0_.1, ...), custom_call_target="tpu_custom_call" | custom-call | tf_op jit(solution)/shard_map/pallas_call | solution.py:341
  208.5 1.4 collective-permute-start
  209.9 10.4 %shard_map.188 = (bf16[2,512,4096]{2,1,0:T(8,128)(2,1)}, bf16[2,512,4096]{2,1,0:T(8,128)(2,1)}, bf16[2,4096,512]{2,1,0:T(8,128)(2,1)}, f32[2,64,4096]{2,1,0:T(8,...) custom-call(bf16[2,512,4096]{2,1,0:T(8,128)(2,1)S(1)} %get-tuple-element.31.refs_0_, ...), custom_call_target="tpu_custom_call" | custom-call | bytes 62914560 | tf_op jit(solution)/shard_map/pallas_call | solution.py:377
  220.3 2.2 collective-permute-done.refs_4_
  222.5 2.2 collective-permute-start.1
  224.8 3.0 %shard_map.189 = (f32[2,64,4096]{2,1,0:T(8,128)}, f32[2,64,4096]{2,1,0:T(8,128)}, f32[2,512,512]{2,1,0:T(8,128)}, bf16[2,4096,512]{2,1,0:T(8,128)(2,1)}) custom-call(f32[2,64,4096]{2,1,0:T(8,128)S(1)} %get-tuple-element.39.refs_0_, f32[2,64,4096]{2,1,0:T(8,128)S(1)} %get-tuple-element.40.refs_1_, ...), custom_call_target="tpu_custom_call", output_to_operand_aliasing={{3}: (3, {})} | custom-call | bytes 14680064 | tf_op jit(solution)/shard_map/pallas_call | solution.py:377
  227.8 0.0 collective-permute-done.1.refs_1_
  227.8 1.0 shard_map.190
Async XLA Ops:
  208.5 14.0 %collective-permute-start = (bf16[1024,512]{1,0:T(8,128)(2,1)S(1)}, bf16[1024,512]{1,0:T(8,128)(2,1)S(1)}, u32[]{:S(2)}, u32[]{:S(2)}) collective-permute-start(bf16[1024,512]{1,0:T(8,128)(2,1)S(1)} %get-tuple-element.42), channel_id=1, source_target_pairs={{0,2},{1,7},{2,4},{3,1},{4,6},{5,3},{6,0},{7,5},{8,10},{9,15},{10,... | collective-permute-start | bytes 3145736 | tf_op jit(solution)/shard_map/ppermute | solution.py:392
  222.5 5.2 %collective-permute-start.1 = (bf16[1024,512]{1,0:T(8,128)(2,1)S(1)}, bf16[1024,512]{1,0:T(8,128)(2,1)S(1)}, u32[]{:S(2)}, u32[]{:S(2)}) collective-permute-start(bf16[1024,512]{1,0:T(8,128)(2,1)S(1)} %collective-permute-done.refs_4_), channel_id=1, source_target_pairs={{0,1},{1,0},{2,3},{3,2},{4,5},{5,4},{6,7},{7,6},{8,9},{9,8},{10,11... | collective-permute-start | bytes 3145736 | tf_op jit(solution)/shard_map/ppermute | solution.py:396

commit v5 on v4

--- a/solution.py
+++ b/solution.py
@@ -10,16 +10,16 @@
 MESH = pl.DeviceIdType.MESH
 CORES = 2
 PIECES = 8
-LAST_PIECES = 4
 TILE = (16, 512)
 WAYS = (0, 1)
 F32, BF16 = jnp.float32, jnp.bfloat16
+FIRST = range(8)
 VMEM_LIMIT = 16 * 2**20
 
 
 def kernel(n, fine, *refs):
     g, w, m_in, v_in, new, m, v = (refs[i : i + 3] for i in range(0, 21, 3))
-    tail, *refs = refs[21:]
+    tail, last, *refs = refs[21:]
     far, near, own_w = (refs[i : i + 3] for i in range(0, 9, 3))
     (stage, acc, squares, term_sem, mate_sem, head_sem, stage_sem, state_sem, first_sem, second_sem, last_sem,
      back_sem, mate_send, back_send, sum_send, ring_send, square_sem, tail_sem) = refs[9:]
@@ -267,19 +267,12 @@
                 pltpu.make_async_remote_copy(
                     src_ref=here, dst_ref=here, send_sem=tail_sem.at[2], recv_sem=tail_sem.at[way], **to(mate)).start()
 
-    def last_pieces(k, a, body):
-        if k < final - 1:
-            body(0, 0, height[a])
-        else:
-            size = height[a] // LAST_PIECES
-            pl.loop(0, LAST_PIECES)(lambda q: body(q, q * size, size))
-
     for k, a, l in steps[:final]:
-        def body(q, start, size):
-            for way in WAYS:
-                ring(way, a, source[way], way * half + l, start, size, last_sem.at[way, k + q])
-
-        last_pieces(k, a, body)
+        for way in WAYS:
+            here = new[a].at[way * half + l, block(a, source[way]), :]
+            there = last.at[way] if k == final - 1 else here
+            pltpu.make_async_remote_copy(
+                src_ref=here, dst_ref=there, send_sem=ring_send.at[way, a], recv_sem=last_sem.at[way, k], **to(side[way])).start()
     for k, a, l in steps:
         for way in WAYS:
             layer = (1 - way) * half + l
@@ -292,30 +285,30 @@
     where = pl.ds(pl.multiple_of((left_chip + core * (right_chip - left_chip)) * pair, pair), pair)
     to_tail = pltpu.make_async_copy(new[a].at[core * half + l, where, :], tail, tail_sem.at[3])
     to_tail.start()
-    for k, a, l in steps[:final]:
-        def body(q, start, size):
-            for way in WAYS:
-                layer = way * half + l
-                drain(last_sem.at[way, k + q], new[a].at[layer, block(a, mine(far_chip), start, size), :])
-                back(a, mine(far_chip), layer, start, size)
-
-        last_pieces(k, a, body)
+    for k, a, l in steps[: final - 1]:
+        for way in WAYS:
+            layer = way * half + l
+            drain(last_sem.at[way, k], new[a].at[layer, block(a, mine(far_chip)), :])
+            back(a, mine(far_chip), layer, 0, height[a])
     to_tail.wait()
     drain(tail_sem.at[2], new[fine].at[0, pl.ds(0, 2 * height[fine]), :])
     for a in arrays:
         drain(mate_send.at[a], new[a].at[:half])
+        blocks = (4 * layers - (4 if a == fine else 2 if a == steps[final - 1][1] else 0)) // half
         for sem in (back_send, back_sem):
-            drain(sem.at[a], new[a].at[:half] if a != fine else new[a].at[: layers - 1, pl.ds(0, 4 * height[a]), :])
+            drain(sem.at[a], new[a].at[:half, pl.ds(0, blocks * height[a]), :])
         for way in WAYS:
             blocks = 3 * half - (a == fine)
             drain(ring_send.at[way, a], new[a].at[0, pl.ds(0, blocks * height[a]), :])
+    for way in WAYS:
+        drain(last_sem.at[way, final - 1], last.at[way])
     drain(square_sem.at[0], squares.at[pl.ds(0, n - 1)])
 
 
 def solution(mesh):
     n = mesh.shape["dp"]
     chips = n // CORES
-    onward = [(i, (i // CORES + (1 if i % CORES == 0 else chips - 1)) % chips * CORES + i % CORES) for i in range(n)]
+    onward = [(i, (i // CORES + (1 if i % CORES == 0 else chips - 1)) % chips * CORES + 1 - i % CORES) for i in range(n)]
     mates = [(i, i // CORES * CORES + 1 - i % CORES) for i in range(n)]
 
     def step(*arrays):
@@ -338,66 +331,75 @@
             + [dma((2, steps)), dma((2, steps)), dma((2, steps - 1 + PIECES))]
             + [dma((3,)), dma((3,)), dma((3,)), dma((2, 3)), dma((2, 3)), dma((2,)), dma((4,))]
         )
-        *results, tail = pl.pallas_call(
+        late = [a for a in range(3) if a != fine][-1]
+        *results, tail, last = pl.pallas_call(
             functools.partial(kernel, n, fine),
-            out_shape=[pltpu.VMEM(shape, dtype) for shape, dtype in [*out, ((CORES * rows, columns), BF16)]],
+            out_shape=[pltpu.VMEM(shape, dtype) for shape, dtype in [*out, ((CORES * rows, columns), BF16), ((2, *blocks[late]), BF16)]],
             in_specs=[hbm] * len(arrays),
-            out_specs=[vmem] * (len(out) + 1),
+            out_specs=[vmem] * (len(out) + 2),
             scratch_shapes=scratch,
             compiler_params=pltpu.CompilerParams(
                 collective_id=0, has_side_effects=True, vmem_limit_bytes=VMEM_LIMIT),
         )(*arrays)
 
-        def held(x):
-            return pltpu.with_memory_space_constraint(x, pltpu.VMEM)
-
-        def write(indices, place=None, part=None, whole=None):
-            sources = [held(results[i]) for i in indices]
-            shapes = [jax.ShapeDtypeStruct(*out[i]) for i in indices]
-            specs, aliases = [vmem] * len(indices), {}
-            if part is not None:
-                aliases = {len(sources): len(shapes)}
-                sources += [whole, held(part)]
-                shapes.append(jax.ShapeDtypeStruct(*out[fine]))
-                specs = specs + [hbm, vmem]
+        def write(done, indices, patches=()):
+            held = [pltpu.with_memory_space_constraint(x, pltpu.VMEM) for x in (*(results[i] for i in indices), *(p[1] for p in patches))]
+            changed = sorted({p[0] for p in patches})
+            written = [*changed, *indices]
 
             def body(*refs):
-                ins, outs, sem = refs[: len(sources)], refs[len(sources) : -1], refs[-1]
-                copies = [pltpu.make_async_copy(ins[i], outs[i], sem.at[i]) for i in range(len(indices))]
-                if part is not None:
-                    layer, first = place(lax.axis_index("dp"))
-                    to = outs[-1].at[layer, pl.ds(pl.multiple_of(first, CORES * rows), CORES * rows), :]
-                    copies.append(pltpu.make_async_copy(ins[-1], to, sem.at[len(indices)]))
+                olds, refs = refs[: len(changed)], refs[len(changed) :]
+                ins, outs, sem = refs[: len(held)], dict(zip(written, refs[len(held) : -1], strict=True)), refs[-1]
+                to = [outs[i] for i in indices] + [place(outs[i]) for i, _, place in patches]
+                copies = [pltpu.make_async_copy(x, y, sem.at[i]) for i, (x, y) in enumerate(zip(ins, to, strict=True))]
                 for copy in copies:
                     copy.start()
                 for copy in copies:
                     copy.wait()
 
-            moved = sum(x.size * x.dtype.itemsize for x in (*(results[i] for i in indices), *(() if part is None else (part,))))
-            return pl.pallas_call(
+            fresh = pl.pallas_call(
                 body,
-                out_shape=shapes,
-                in_specs=specs,
-                out_specs=[hbm] * len(shapes),
-                scratch_shapes=[dma((len(shapes),))],
-                input_output_aliases=aliases,
+                out_shape=[jax.ShapeDtypeStruct(*out[i]) for i in written],
+                in_specs=[hbm] * len(changed) + [vmem] * len(held),
+                out_specs=[hbm] * len(written),
+                scratch_shapes=[dma((len(held),))],
+                input_output_aliases={i: i for i in range(len(changed))},
                 compiler_params=pltpu.CompilerParams(vmem_limit_bytes=VMEM_LIMIT),
-                cost_estimate=pl.CostEstimate(flops=0, bytes_accessed=2 * moved, transcendentals=0),
-            )(*sources)
-
-        def place_of(me, core):
-            far_chip = lax.rem(me // CORES + chips // 2, chips)
-            return core * (layers // 2) + layers // 2 - 1, far_chip * CORES * rows
-
+                cost_estimate=pl.CostEstimate(
+                    flops=0, bytes_accessed=2 * sum(x.size * x.dtype.itemsize for x in held), transcendentals=0),
+            )(*(done[i] for i in changed), *held)
+            done.update(zip(written, fresh, strict=True))
+
+        def far_rows(of_mate):
+            me = lax.axis_index("dp")
+            core = me % CORES
+            return lax.rem(me // CORES + chips // 2, chips), (1 - core if of_mate else core)
+
+        def from_tail(of_mate):
+            def place(ref):
+                far_chip, core = far_rows(of_mate)
+                pair = CORES * rows
+                return ref.at[(CORES - core) * (layers // 2) - 1, pl.ds(pl.multiple_of(far_chip * pair, pair), pair), :]
+
+            return place
+
+        def from_last(of_mate):
+            def place(ref):
+                far_chip, core = far_rows(of_mate)
+                size = blocks[late][0]
+                return ref.at[layers // 2 - 1 :: layers // 2, pl.ds(pl.multiple_of((far_chip * CORES + core) * size, size), size), :]
+
+            return place
+
+        done = {}
         own = lax.ppermute(tail, "dp", onward)
-        first = list(range(6))
-        done = dict(zip(first, write(first), strict=True))
+        mates_last = lax.ppermute(last, "dp", mates)
+        write(done, FIRST)
         own, done[fine] = lax.optimization_barrier((own, done[fine]))
-        mates_part = lax.ppermute(own, "dp", mates)
-        later = list(range(6, 9))
-        *got, whole = write(later, lambda me: place_of(me, lax.rem(me, CORES)), own, done[fine])
-        done.update(zip(later, got, strict=True))
-        (done[fine],) = write([], lambda me: place_of(me, 1 - lax.rem(me, CORES)), mates_part, whole)
+        mates_own = lax.ppermute(own, "dp", mates)
+        write(done, [i for i in range(9) if i not in FIRST],
+              [(fine, own, from_tail(False)), (late, last, from_last(False)), (late, mates_last, from_last(True))])
+        write(done, [], [(fine, mates_own, from_tail(True))])
         return tuple(done[i] for i in range(9))
 
     all_of, cut = P(None, None, None), P(None, "dp", None)

time: 229 us -> 226 us (0.987)
  transfers between devices with their start and end apart: 2 -> 3, of which waited for: 1 -> 2; matrix products, arithmetic and copies ran while one was open for 0% -> 0% of each run, Pallas kernels for 6% -> 6%
where the time goes in v5:
time: 226 us
  Pallas kernels  221 us (98%)
  starting transfers between devices  2.39 us (1%)
    pallas_call x1, Pallas kernels, step(): pl.pallas_call(functools.partial(kernel, n, fine), out_shape=[pltpu.VMEM(...  206 us
    pallas_call x3, Pallas kernels, write(): pl.pallas_call(body, out_shape=[jax.ShapeDtypeStruct(*out[i]) for i in wr...  15.1 us
  transfers between devices with their start and end apart: 3, of which 2 were waited for; matrix products, arithmetic and copies ran while one was open for 0% of the time, Pallas kernels for 6%

profile of v5, /device:TPU:113, one launch (start us, length us, event | category | flops | bytes accessed | tf_op | source)
XLA Modules:
  0.0 225.7 jit_solution(12415760253158349418)
XLA Ops:
  0.6 205.9 %shard_map.187 = (bf16[2,512,4096]{2,1,0:T(8,128)(2,1)S(1)}, bf16[2,512,4096]{2,1,0:T(8,128)(2,1)S(1)}, bf16[2,4096,512]{2,1,0:T(8,128)(2,1)S(1)}, f32[2,64,4096...) custom-call(bf16[1,2,512,4096]{3,2,1,0:T(8,128)(2,1)} %refs_0_.1, ...), custom_call_target="tpu_custom_call" | custom-call | tf_op jit(solution)/shard_map/pallas_call | solution.py:335
  206.5 2.4 %collective-permute-start = (bf16[1024,512]{1,0:T(8,128)(2,1)S(1)}, bf16[1024,512]{1,0:T(8,128)(2,1)S(1)}, u32[]{:S(2)}, u32[]{:S(2)}) collective-permute-start(bf16[1024,512]{1,0:T(8,128)(2,1)S(1)} %get-tuple-element.43), channel_id=1, source_target_pairs={{0,3},{1,6},{2,5},{3,0},{4,7},{5,2},{6,1},{7,4},{8,11},{9,14},{10,... | collective-permute-start | bytes 3145736 | tf_op jit(solution)/shard_map/ppermute | solution.py:395
  208.9 0.0 collective-permute-start.1
  208.9 11.7 %shard_map.188 = (bf16[2,512,4096]{2,1,0:T(8,128)(2,1)}, bf16[2,512,4096]{2,1,0:T(8,128)(2,1)}, bf16[2,4096,512]{2,1,0:T(8,128)(2,1)}, f32[2,64,4096]{2,1,0:T(8,...) custom-call(bf16[2,512,4096]{2,1,0:T(8,128)(2,1)S(1)} %get-tuple-elemen, ...), custom_call_target="tpu_custom_call" | custom-call | bytes 71303168 | tf_op jit(solution)/shard_map/pallas_call | solution.py:360
  220.6 1.4 collective-permute-done.refs_3_
  222.0 0.0 collective-permute-start.2
  222.0 0.0 collective-permute-done.1.refs_5_
  222.0 2.4 %shard_map.189 = (bf16[2,512,4096]{2,1,0:T(8,128)(2,1)}, bf16[2,4096,512]{2,1,0:T(8,128)(2,1)}, f32[2,512,512]{2,1,0:T(8,128)}) custom-call(bf16[2,512,4096]{2,1,0:T(8,128)(2,1)} %get-tuple-element.42.refs_0_, bf16[2,4096,512]{2,1,0:T(8,128)(2,1)} %get-tuple-element.45.refs_1_, ...), custom_call_target="tpu_custom_call", output_to_operand_aliasing={{0}: (0, {}), {1}: (1, {})} | custom-call | bytes 10485760 | tf_op jit(solution)/shard_map/pallas_call | solution.py:360
  224.4 0.3 collective-permute-done.2.refs_1_
  224.7 1.0 shard_map.190
Async XLA Ops:
  206.5 15.5 %collective-permute-start = (bf16[1024,512]{1,0:T(8,128)(2,1)S(1)}, bf16[1024,512]{1,0:T(8,128)(2,1)S(1)}, u32[]{:S(2)}, u32[]{:S(2)}) collective-permute-start(bf16[1024,512]{1,0:T(8,128)(2,1)S(1)} %get-tuple-element.43), channel_id=1, source_target_pairs={{0,3},{1,6},{2,5},{3,0},{4,7},{5,2},{6,1},{7,4},{8,11},{9,14},{10,... | collective-permute-start | bytes 3145736 | tf_op jit(solution)/shard_map/ppermute | solution.py:395
  208.9 13.1 %collective-permute-start.1 = (bf16[2,64,4096]{2,1,0:T(8,128)(2,1)S(1)}, bf16[2,64,4096]{2,1,0:T(8,128)(2,1)S(1)}, u32[]{:S(2)}, u32[]{:S(2)}) collective-permute-start(bf16[2,64,4096]{2,1,0:T(8,128)(2,1)S(1)} %get-tuple-element.48.refs_4_), channel_id=1, source_target_pairs={{0,1},{1,0},{2,3},{3,2},{4,5},{5,4},{6,7},{7,6},{8,9},{9,8},{10,11... | collective-permute-start | bytes 3145736 | tf_op jit(solution)/shard_map/ppermute | solution.py:396
  222.0 2.7 %collective-permute-start.2 = (bf16[1024,512]{1,0:T(8,128)(2,1)S(1)}, bf16[1024,512]{1,0:T(8,128)(2,1)S(1)}, u32[]{:S(2)}, u32[]{:S(2)}) collective-permute-start(bf16[1024,512]{1,0:T(8,128)(2,1)S(1)} %collective-permute-done.refs_3_), channel_id=1, source_target_pairs={{0,1},{1,0},{2,3},{3,2},{4,5},{5,4},{6,7},{7,6},{8,9},{9,8},{10,11... | collective-permute-start | bytes 3145736 | tf_op jit(solution)/shard_map/ppermute | solution.py:399

commit v6 on v5

--- a/solution.py
+++ b/solution.py
@@ -1,4 +1,5 @@
 import functools
+import math
 
 import jax
 import jax.numpy as jnp
@@ -9,7 +10,7 @@
 
 MESH = pl.DeviceIdType.MESH
 CORES = 2
-PIECES = 8
+PIECES = (16, 16, 8, 4, 2)
 TILE = (16, 512)
 WAYS = (0, 1)
 F32, BF16 = jnp.float32, jnp.bfloat16
@@ -21,8 +22,8 @@
     g, w, m_in, v_in, new, m, v = (refs[i : i + 3] for i in range(0, 21, 3))
     tail, last, *refs = refs[21:]
     far, near, own_w = (refs[i : i + 3] for i in range(0, 9, 3))
-    (stage, acc, squares, term_sem, mate_sem, head_sem, stage_sem, state_sem, first_sem, second_sem, last_sem,
-     back_sem, mate_send, back_send, sum_send, ring_send, square_sem, tail_sem) = refs[9:]
+    (stage, acc, squares, load_sem, mate_sem, head_sem, stage_sem, first_sem, second_sem, last_sem, back_sem, mate_send,
+     back_send, sum_send, ring_send, square_sem, tail_sem) = refs[9:]
 
     chips = n // CORES
     me = lax.axis_index("dp")
@@ -50,14 +51,13 @@
 
     def block(a, index, start=0, size=None):
         size = size or height[a]
-        return pl.ds(pl.multiple_of(index * height[a] + start, size), size)
-
-    def pieces(k, a, body):
-        if k < final:
-            body(0, 0, height[a])
-        else:
-            size = height[a] // PIECES
-            pl.loop(0, PIECES)(lambda q: body(q, q * size, size))
+        return pl.ds(pl.multiple_of(index * height[a] + start, math.gcd(height[a], start)), size)
+
+    def pieces(k, a, order=1):
+        sizes = [height[a] // p for p in PIECES[::order]] if k == final else [height[a]]
+        return [(q, sum(sizes[:q]), size) for q, size in enumerate(sizes)]
+
+    head = pieces(final, fine)
 
     def tiles(a, size, body, carry):
         columns = m[a].shape[2] // TILE[1]
@@ -76,38 +76,48 @@
 
     targets = (far_chip, right_chip, left_chip, chip)
 
+    def group(t, a):
+        return (0 if a == fine else 1) if t == 0 else 2 if t < 3 else 3
+
     def term(t, a):
         where = block(a, mine(targets[t]))
-        return pltpu.make_async_copy(g[a].at[0, :, where, :], new[a].at[:, where, :], term_sem.at[t, a])
+        return pltpu.make_async_copy(g[a].at[0, :, where, :], new[a].at[:, where, :], load_sem.at[group(t, a)])
 
     def mate_term(t, a):
         return pltpu.make_async_remote_copy(
             src_ref=g[a].at[0, :, block(a, mates(targets[t])), :], dst_ref=new[a].at[:, block(a, mine(targets[t])), :],
-            send_sem=mate_send.at[a], recv_sem=mate_sem.at[t, a], **to(mate))
-
-    def mate_head(q):
-        size = height[fine] // PIECES
+            send_sem=mate_send.at[a], recv_sem=mate_sem.at[group(t, a)], **to(mate))
+
+    def mate_head(q, start, size):
         return pltpu.make_async_remote_copy(
-            src_ref=stage.at[:, block(fine, 0, q * size, size), :],
-            dst_ref=new[fine].at[:, block(fine, mine(far_chip), q * size, size), :],
+            src_ref=stage.at[:, pl.ds(start, size), :],
+            dst_ref=new[fine].at[:, block(fine, mine(far_chip), start, size), :],
             send_sem=mate_send.at[fine], recv_sem=head_sem.at[q], **to(mate))
 
-    to_stage = pltpu.make_async_copy(g[fine].at[0, :, block(fine, mates(far_chip)), :], stage, stage_sem.at[0])
+    def to_stage(q, start, size):
+        return pltpu.make_async_copy(
+            g[fine].at[0, :, block(fine, mates(far_chip), start, size), :], stage.at[:, pl.ds(start, size), :], stage_sem.at[q])
+
+    staged = [(0, *head[0][1:]), (1, head[1][1], height[fine] - head[1][1])]
 
     def states(a):
-        return (pltpu.make_async_copy(m_in[a], m[a], state_sem.at[0, a]),
-                pltpu.make_async_copy(v_in[a], v[a], state_sem.at[1, a]),
-                pltpu.make_async_copy(w[a].at[:, block(a, me), :], own_w[a], state_sem.at[2, a]))
-
+        return (pltpu.make_async_copy(m_in[a], m[a], load_sem.at[4]),
+                pltpu.make_async_copy(v_in[a], v[a], load_sem.at[5]),
+                pltpu.make_async_copy(w[a].at[:, block(a, me), :], own_w[a], load_sem.at[6]))
+
+    for q, start, size in staged:
+        to_stage(q, start, size).start()
     barrier = pltpu.get_barrier_semaphore()
     for o in range(1, n):
         pl.semaphore_signal(barrier, inc=1, **to(lax.rem(me + o, n)))
-    to_stage.start()
     for a in (fine, *arrays[:-1]):
         term(0, a).start()
-    to_stage.wait()
+    to_stage(*staged[0]).wait()
     pl.semaphore_wait(barrier, n - 1)
-    pl.loop(0, PIECES)(lambda q: mate_head(q).start())
+    mate_head(*head[0]).start()
+    to_stage(*staged[1]).wait()
+    for piece in head[1:]:
+        mate_head(*piece).start()
     for t, a in [(0, a) for a in arrays[:-1]] + [(t, a) for a in arrays for t in (1, 2)] + [(3, a) for a in arrays]:
         mate_term(t, a).start()
         if t > 0:
@@ -117,16 +127,19 @@
             copy.start()
     acc[...] = jnp.zeros_like(acc)
 
+    def drain_blocks(sem, count):
+        drain(sem, new[fine].at[:, pl.ds(0, count * height[fine] // layers), :])
+
     arrived = set()
 
     def await_terms(t, a):
-        if (t, a) not in arrived:
-            arrived.add((t, a))
-            term(t, a).wait()
-            if (t, a) == (0, fine):
-                return lambda q: mate_head(q).wait_recv()
-            mate_term(t, a).wait_recv()
-        return lambda q: None
+        i = group(t, a)
+        if i not in arrived:
+            arrived.add(i)
+            count = layers * sum(group(t, a) == i for t in range(4) for a in arrays)
+            drain_blocks(load_sem.at[i], count)
+            if i > 0:
+                drain_blocks(mate_sem.at[i], count)
 
     def total(t, a, layer, at, start, more):
         out = new[a][(layer, *at(mine(targets[t]) * height[a] + start))].astype(F32)
@@ -145,47 +158,36 @@
 
     def send_sum(way, a, src, dst, sem):
         pltpu.make_async_remote_copy(
-            src_ref=src, dst_ref=dst, send_sem=sum_send.at[way, a], recv_sem=sem, **to(side[way])).start()
-
-    def part(a, start, size):
-        return pl.ds(pl.multiple_of(start, size), size)
+            src_ref=src, dst_ref=dst, send_sem=sum_send.at[a], recv_sem=sem, **to(side[way])).start()
 
     for k, a, l in head_first:
-        here = await_terms(0, a)
-
-        def body(q, start, size):
-            here(q)
+        await_terms(0, a)
+        for q, start, size in pieces(k, a):
+            if a == fine and k == final:
+                mate_head(q, start, size).wait_recv()
             for way in WAYS:
                 src = summed(0, a, way * half + l, start, size)
-                send_sum(way, a, src, far[a].at[way, l, part(a, start, size), :], first_sem.at[way, k])
-
-        pieces(k, a, body)
+                send_sum(way, a, src, far[a].at[way, l, pl.ds(start, size), :], first_sem.at[k])
     for k, a, l in steps:
         for way in WAYS:
             await_terms(1 + way, a)
             layer = (1 - way) * half + l
             src = summed(1 + way, a, layer, 0, height[a])
-            send_sum(way, a, src, near[a].at[way, layer], second_sem.at[way, k])
+            send_sum(way, a, src, near[a].at[way, layer], second_sem.at[k])
     for k, a, l in steps:
-        for way in WAYS:
-            drain(first_sem.at[way, k], far[a].at[way, l])
-
-        def body(q, start, size):
+        drain(first_sem.at[k], far[a].at[:, l])
+        for q, start, size in pieces(k, a, -1):
             for way in WAYS:
                 layer = way * half + l
                 src = summed(1 + way, a, layer, start, size, [(far[a], (way, l))])
-                send_sum(way, a, src, near[a].at[way, layer, part(a, start, size), :], last_sem.at[way, k + q])
-
-        pieces(k, a, body)
+                send_sum(way, a, src, near[a].at[way, layer, pl.ds(start, size), :], last_sem.at[k + q])
     for k, a, l in steps:
         await_terms(3, a)
-        for way in WAYS:
-            drain(second_sem.at[way, k], near[a].at[way, (1 - way) * half + l])
-
-        def body(q, start, size):
+        drain(second_sem.at[k], far[a].at[:, l])
+        for q, start, size in pieces(k, a, -1):
+            drain(last_sem.at[k + q], far[a].at[:, l, pl.ds(start, size), :])
             for way in WAYS:
                 layer = way * half + l
-                drain(last_sem.at[way, k + q], near[a].at[way, layer, part(a, start, size), :])
 
                 def tile(at, carry):
                     rounded = total(3, a, layer, at, start, [(near[a], (i, layer)) for i in WAYS]).astype(BF16)
@@ -199,19 +201,15 @@
 
                 acc[...] = tiles(a, size, tile, acc[...])
 
-        pieces(k, a, body)
-
     squares[me] = acc[...]
-    for way in WAYS:
-        for a in arrays:
-            drain(sum_send.at[way, a], new[a].at[:half, pl.ds(0, 3 * height[a]), :])
+    for a in arrays:
+        drain_blocks(sum_send.at[a], 3 * layers)
     for o in range(1, n):
         pltpu.make_async_remote_copy(
             src_ref=squares.at[me], dst_ref=squares.at[me], send_sem=square_sem.at[0], recv_sem=square_sem.at[1],
             **to(lax.rem(me + o, n))).start()
-    for a in arrays:
-        for copy in states(a):
-            copy.wait()
+    for i, ref in ((4, F32), (5, F32), (6, BF16)):
+        drain_blocks(load_sem.at[i], len(arrays) * layers * (2 if ref == F32 else 1))
     drain(square_sem.at[1], squares.at[pl.ds(0, n - 1)])
     everyone = squares[0]
     for i in range(1, n):
@@ -223,7 +221,7 @@
     def ring(way, a, index, layer, start, size, sem):
         here = new[a].at[layer, block(a, index, start, size), :]
         pltpu.make_async_remote_copy(
-            src_ref=here, dst_ref=here, send_sem=ring_send.at[way, a], recv_sem=sem, **to(side[way])).start()
+            src_ref=here, dst_ref=here, send_sem=ring_send.at[a], recv_sem=sem, **to(side[way])).start()
 
     def back(a, index, layer, start, size):
         here = new[a].at[layer, block(a, index, start, size), :]
@@ -231,7 +229,7 @@
             src_ref=here, dst_ref=here, send_sem=back_send.at[a], recv_sem=back_sem.at[a], **to(mate)).start()
 
     for k, a, l in head_first:
-        def body(q, start, size):
+        for q, start, size in pieces(k, a):
             for way in WAYS:
                 layer = way * half + l
 
@@ -248,18 +246,16 @@
                     return carry
 
                 tiles(a, size, tile, 0)
-                ring(way, a, me, layer, start, size, first_sem.at[way, k])
+                ring(way, a, me, layer, start, size, first_sem.at[k])
                 back(a, me, layer, start, size)
-
-        pieces(k, a, body)
     for k, a, l in steps:
         for way in WAYS:
-            ring(way, a, me, (1 - way) * half + l, 0, height[a], second_sem.at[way, k])
+            ring(way, a, me, (1 - way) * half + l, 0, height[a], second_sem.at[k])
     source = (mine(left_chip), mine(right_chip))
     for k, a, l in head_first:
+        drain(first_sem.at[k], far[a].at[:, l])
         for way in WAYS:
             layer = way * half + l
-            drain(first_sem.at[way, k], new[a].at[layer, block(a, source[way]), :])
             if k < final:
                 back(a, source[way], layer, 0, height[a])
             else:
@@ -272,11 +268,11 @@
             here = new[a].at[way * half + l, block(a, source[way]), :]
             there = last.at[way] if k == final - 1 else here
             pltpu.make_async_remote_copy(
-                src_ref=here, dst_ref=there, send_sem=ring_send.at[way, a], recv_sem=last_sem.at[way, k], **to(side[way])).start()
+                src_ref=here, dst_ref=there, send_sem=ring_send.at[a], recv_sem=last_sem.at[k], **to(side[way])).start()
     for k, a, l in steps:
+        drain(second_sem.at[k], far[a].at[:, l])
         for way in WAYS:
             layer = (1 - way) * half + l
-            drain(second_sem.at[way, k], new[a].at[layer, block(a, source[way]), :])
             back(a, source[way], layer, 0, height[a])
     _, a, l = steps[final]
     for way in WAYS:
@@ -286,9 +282,9 @@
     to_tail = pltpu.make_async_copy(new[a].at[core * half + l, where, :], tail, tail_sem.at[3])
     to_tail.start()
     for k, a, l in steps[: final - 1]:
+        drain(last_sem.at[k], far[a].at[:, l])
         for way in WAYS:
             layer = way * half + l
-            drain(last_sem.at[way, k], new[a].at[layer, block(a, mine(far_chip)), :])
             back(a, mine(far_chip), layer, 0, height[a])
     to_tail.wait()
     drain(tail_sem.at[2], new[fine].at[0, pl.ds(0, 2 * height[fine]), :])
@@ -297,11 +293,8 @@
         blocks = (4 * layers - (4 if a == fine else 2 if a == steps[final - 1][1] else 0)) // half
         for sem in (back_send, back_sem):
             drain(sem.at[a], new[a].at[:half, pl.ds(0, blocks * height[a]), :])
-        for way in WAYS:
-            blocks = 3 * half - (a == fine)
-            drain(ring_send.at[way, a], new[a].at[0, pl.ds(0, blocks * height[a]), :])
-    for way in WAYS:
-        drain(last_sem.at[way, final - 1], last.at[way])
+        drain_blocks(ring_send.at[a], 3 * layers - (2 if a == fine else 0))
+    drain(last_sem.at[final - 1], last)
     drain(square_sem.at[0], squares.at[pl.ds(0, n - 1)])
 
 
@@ -327,9 +320,9 @@
             + [pltpu.VMEM((2, layers, *b), BF16) for b in blocks]
             + [pltpu.VMEM((layers, *b), BF16) for b in blocks]
             + [pltpu.VMEM((layers, *blocks[fine]), BF16), pltpu.VMEM((8, 128), F32), pltpu.VMEM((n, 8, 128), F32)]
-            + [dma((4, 3)), dma((4, 3)), dma((PIECES,)), dma((1,)), dma((3, 3))]
-            + [dma((2, steps)), dma((2, steps)), dma((2, steps - 1 + PIECES))]
-            + [dma((3,)), dma((3,)), dma((3,)), dma((2, 3)), dma((2, 3)), dma((2,)), dma((4,))]
+            + [dma((7,)), dma((4,)), dma((len(PIECES),)), dma((2,))]
+            + [dma((steps,)), dma((steps,)), dma((steps - 1 + len(PIECES),))]
+            + [dma((3,)), dma((3,)), dma((3,)), dma((3,)), dma((3,)), dma((2,)), dma((4,))]
         )
         late = [a for a in range(3) if a != fine][-1]
         *results, tail, last = pl.pallas_call(

time: 226 us -> 225 us (level)
  no operation moved by 1% of the time
where the time goes in v6:
time: 225 us
  Pallas kernels  220 us (98%)
  starting transfers between devices  2.51 us (1%)
    pallas_call x1, Pallas kernels, step(): pl.pallas_call(functools.partial(kernel, n, fine), out_shape=[pltpu.VMEM(...  205 us
    pallas_call x3, Pallas kernels, write(): pl.pallas_call(body, out_shape=[jax.ShapeDtypeStruct(*out[i]) for i in wr...  15.1 us
  transfers between devices with their start and end apart: 3, of which 2 were waited for; matrix products, arithmetic and copies ran while one was open for 0% of the time, Pallas kernels for 6%

profile of v6, /device:TPU:113, one launch (start us, length us, event | category | flops | bytes accessed | tf_op | source)
XLA Modules:
  0.0 224.9 jit_solution(5949619115695209571)
XLA Ops:
  0.6 205.1 %shard_map.187 = (bf16[2,512,4096]{2,1,0:T(8,128)(2,1)S(1)}, bf16[2,512,4096]{2,1,0:T(8,128)(2,1)S(1)}, bf16[2,4096,512]{2,1,0:T(8,128)(2,1)S(1)}, f32[2,64,4096...) custom-call(bf16[1,2,512,4096]{3,2,1,0:T(8,128)(2,1)} %refs_0_.1, ...), custom_call_target="tpu_custom_call" | custom-call | tf_op jit(solution)/shard_map/pallas_call | solution.py:328
  205.7 2.5 %collective-permute-start = (bf16[1024,512]{1,0:T(8,128)(2,1)S(1)}, bf16[1024,512]{1,0:T(8,128)(2,1)S(1)}, u32[]{:S(2)}, u32[]{:S(2)}) collective-permute-start(bf16[1024,512]{1,0:T(8,128)(2,1)S(1)} %get-tuple-element.43), channel_id=1, source_target_pairs={{0,3},{1,6},{2,5},{3,0},{4,7},{5,2},{6,1},{7,4},{8,11},{9,14},{10,... | collective-permute-start | bytes 3145736 | tf_op jit(solution)/shard_map/ppermute | solution.py:388
  208.2 0.0 collective-permute-start.1
  208.2 11.7 %shard_map.188 = (bf16[2,512,4096]{2,1,0:T(8,128)(2,1)}, bf16[2,512,4096]{2,1,0:T(8,128)(2,1)}, bf16[2,4096,512]{2,1,0:T(8,128)(2,1)}, f32[2,64,4096]{2,1,0:T(8,...) custom-call(bf16[2,512,4096]{2,1,0:T(8,128)(2,1)S(1)} %get-tuple-elemen, ...), custom_call_target="tpu_custom_call" | custom-call | bytes 71303168 | tf_op jit(solution)/shard_map/pallas_call | solution.py:353
  219.9 1.3 collective-permute-done.refs_3_
  221.2 0.0 collective-permute-start.2
  221.2 0.0 collective-permute-done.1.refs_5_
  221.2 2.4 %shard_map.189 = (bf16[2,512,4096]{2,1,0:T(8,128)(2,1)}, bf16[2,4096,512]{2,1,0:T(8,128)(2,1)}, f32[2,512,512]{2,1,0:T(8,128)}) custom-call(bf16[2,512,4096]{2,1,0:T(8,128)(2,1)} %get-tuple-element.42.refs_0_, bf16[2,4096,512]{2,1,0:T(8,128)(2,1)} %get-tuple-element.45.refs_1_, ...), custom_call_target="tpu_custom_call", output_to_operand_aliasing={{0}: (0, {}), {1}: (1, {})} | custom-call | bytes 10485760 | tf_op jit(solution)/shard_map/pallas_call | solution.py:353
  223.6 0.3 collective-permute-done.2.refs_1_
  223.9 1.0 shard_map.190
Async XLA Ops:
  205.7 15.5 %collective-permute-start = (bf16[1024,512]{1,0:T(8,128)(2,1)S(1)}, bf16[1024,512]{1,0:T(8,128)(2,1)S(1)}, u32[]{:S(2)}, u32[]{:S(2)}) collective-permute-start(bf16[1024,512]{1,0:T(8,128)(2,1)S(1)} %get-tuple-element.43), channel_id=1, source_target_pairs={{0,3},{1,6},{2,5},{3,0},{4,7},{5,2},{6,1},{7,4},{8,11},{9,14},{10,... | collective-permute-start | bytes 3145736 | tf_op jit(solution)/shard_map/ppermute | solution.py:388
  208.2 13.0 %collective-permute-start.1 = (bf16[2,64,4096]{2,1,0:T(8,128)(2,1)S(1)}, bf16[2,64,4096]{2,1,0:T(8,128)(2,1)S(1)}, u32[]{:S(2)}, u32[]{:S(2)}) collective-permute-start(bf16[2,64,4096]{2,1,0:T(8,128)(2,1)S(1)} %get-tuple-element.48.refs_4_), channel_id=1, source_target_pairs={{0,1},{1,0},{2,3},{3,2},{4,5},{5,4},{6,7},{7,6},{8,9},{9,8},{10,11... | collective-permute-start | bytes 3145736 | tf_op jit(solution)/shard_map/ppermute | solution.py:389
  221.2 2.7 %collective-permute-start.2 = (bf16[1024,512]{1,0:T(8,128)(2,1)S(1)}, bf16[1024,512]{1,0:T(8,128)(2,1)S(1)}, u32[]{:S(2)}, u32[]{:S(2)}) collective-permute-start(bf16[1024,512]{1,0:T(8,128)(2,1)S(1)} %collective-permute-done.refs_3_), channel_id=1, source_target_pairs={{0,1},{1,0},{2,3},{3,2},{4,5},{5,4},{6,7},{7,6},{8,9},{9,8},{10,11... | collective-permute-start | bytes 3145736 | tf_op jit(solution)/shard_map/ppermute | solution.py:392

commit v7 on v6

--- a/solution.py
+++ b/solution.py
@@ -11,6 +11,7 @@
 MESH = pl.DeviceIdType.MESH
 CORES = 2
 PIECES = (16, 16, 8, 4, 2)
+HOLD = ((0, 3300), (800, 0))
 TILE = (16, 512)
 WAYS = (0, 1)
 F32, BF16 = jnp.float32, jnp.bfloat16
@@ -160,6 +161,12 @@
         pltpu.make_async_remote_copy(
             src_ref=src, dst_ref=dst, send_sem=sum_send.at[a], recv_sem=sem, **to(side[way])).start()
 
+    def hold(phase):
+        for index, time in enumerate(HOLD[phase]):
+            if time:
+                pl.when(core == index)(lambda: pl.delay(time))
+
+    hold(0)
     for k, a, l in head_first:
         await_terms(0, a)
         for q, start, size in pieces(k, a):
@@ -228,6 +235,7 @@
         pltpu.make_async_remote_copy(
             src_ref=here, dst_ref=here, send_sem=back_send.at[a], recv_sem=back_sem.at[a], **to(mate)).start()
 
+    hold(1)
     for k, a, l in head_first:
         for q, start, size in pieces(k, a):
             for way in WAYS:

time: 225 us -> 224 us (level)
  transfers between devices with their start and end apart: 3 -> 3, of which waited for: 2 -> 1; matrix products, arithmetic and copies ran while one was open for 0% -> 0% of each run, Pallas kernels for 6% -> 6%
where the time goes in v7:
time: 224 us
  Pallas kernels  219 us (98%)
  starting transfers between devices  3.57 us (2%)
    pallas_call x1, Pallas kernels, step(): pl.pallas_call(functools.partial(kernel, n, fine), out_shape=[pltpu.VMEM(...  204 us
    pallas_call x3, Pallas kernels, write(): pl.pallas_call(body, out_shape=[jax.ShapeDtypeStruct(*out[i]) for i in wr...  15.1 us
  transfers between devices with their start and end apart: 3, of which 1 were waited for; matrix products, arithmetic and copies ran while one was open for 0% of the time, Pallas kernels for 6%

profile of v7, /device:TPU:113, one launch (start us, length us, event | category | flops | bytes accessed | tf_op | source)
XLA Modules:
  0.0 223.8 jit_solution(6114176674929405943)
XLA Ops:
  0.6 203.7 %shard_map.187 = (bf16[2,512,4096]{2,1,0:T(8,128)(2,1)S(1)}, bf16[2,512,4096]{2,1,0:T(8,128)(2,1)S(1)}, bf16[2,4096,512]{2,1,0:T(8,128)(2,1)S(1)}, f32[2,64,4096...) custom-call(bf16[1,2,512,4096]{3,2,1,0:T(8,128)(2,1)} %refs_0_.1, ...), custom_call_target="tpu_custom_call" | custom-call | tf_op jit(solution)/shard_map/pallas_call | solution.py:336
  204.3 3.3 %collective-permute-start = (bf16[1024,512]{1,0:T(8,128)(2,1)S(1)}, bf16[1024,512]{1,0:T(8,128)(2,1)S(1)}, u32[]{:S(2)}, u32[]{:S(2)}) collective-permute-start(bf16[1024,512]{1,0:T(8,128)(2,1)S(1)} %get-tuple-element.43), channel_id=1, source_target_pairs={{0,3},{1,6},{2,5},{3,0},{4,7},{5,2},{6,1},{7,4},{8,11},{9,14},{10,... | collective-permute-start | bytes 3145736 | tf_op jit(solution)/shard_map/ppermute | solution.py:396
  207.6 0.0 collective-permute-start.1
  207.6 11.7 %shard_map.188 = (bf16[2,512,4096]{2,1,0:T(8,128)(2,1)}, bf16[2,512,4096]{2,1,0:T(8,128)(2,1)}, bf16[2,4096,512]{2,1,0:T(8,128)(2,1)}, f32[2,64,4096]{2,1,0:T(8,...) custom-call(bf16[2,512,4096]{2,1,0:T(8,128)(2,1)S(1)} %get-tuple-elemen, ...), custom_call_target="tpu_custom_call" | custom-call | bytes 71303168 | tf_op jit(solution)/shard_map/pallas_call | solution.py:361
  219.4 0.8 collective-permute-done.refs_3_
  220.1 0.3 collective-permute-start.2
  220.4 0.0 collective-permute-done.1.refs_5_
  220.4 2.4 %shard_map.189 = (bf16[2,512,4096]{2,1,0:T(8,128)(2,1)}, bf16[2,4096,512]{2,1,0:T(8,128)(2,1)}, f32[2,512,512]{2,1,0:T(8,128)}) custom-call(bf16[2,512,4096]{2,1,0:T(8,128)(2,1)} %get-tuple-element.42.refs_0_, bf16[2,4096,512]{2,1,0:T(8,128)(2,1)} %get-tuple-element.45.refs_1_, ...), custom_call_target="tpu_custom_call", output_to_operand_aliasing={{0}: (0, {}), {1}: (1, {})} | custom-call | bytes 10485760 | tf_op jit(solution)/shard_map/pallas_call | solution.py:361
  222.8 0.0 collective-permute-done.2.refs_1_
  222.8 1.0 shard_map.190
Async XLA Ops:
  204.3 15.8 %collective-permute-start = (bf16[1024,512]{1,0:T(8,128)(2,1)S(1)}, bf16[1024,512]{1,0:T(8,128)(2,1)S(1)}, u32[]{:S(2)}, u32[]{:S(2)}) collective-permute-start(bf16[1024,512]{1,0:T(8,128)(2,1)S(1)} %get-tuple-element.43), channel_id=1, source_target_pairs={{0,3},{1,6},{2,5},{3,0},{4,7},{5,2},{6,1},{7,4},{8,11},{9,14},{10,... | collective-permute-start | bytes 3145736 | tf_op jit(solution)/shard_map/ppermute | solution.py:396
  207.6 12.8 %collective-permute-start.1 = (bf16[2,64,4096]{2,1,0:T(8,128)(2,1)S(1)}, bf16[2,64,4096]{2,1,0:T(8,128)(2,1)S(1)}, u32[]{:S(2)}, u32[]{:S(2)}) collective-permute-start(bf16[2,64,4096]{2,1,0:T(8,128)(2,1)S(1)} %get-tuple-element.48.refs_4_), channel_id=1, source_target_pairs={{0,1},{1,0},{2,3},{3,2},{4,5},{5,4},{6,7},{7,6},{8,9},{9,8},{10,11... | collective-permute-start | bytes 3145736 | tf_op jit(solution)/shard_map/ppermute | solution.py:397
  220.1 2.7 %collective-permute-start.2 = (bf16[1024,512]{1,0:T(8,128)(2,1)S(1)}, bf16[1024,512]{1,0:T(8,128)(2,1)S(1)}, u32[]{:S(2)}, u32[]{:S(2)}) collective-permute-start(bf16[1024,512]{1,0:T(8,128)(2,1)S(1)} %collective-permute-done.refs_3_), channel_id=1, source_target_pairs={{0,1},{1,0},{2,3},{3,2},{4,5},{5,4},{6,7},{7,6},{8,9},{9,8},{10,11... | collective-permute-start | bytes 3145736 | tf_op jit(solution)/shard_map/ppermute | solution.py:400

commit v8 on v7

--- a/solution.py
+++ b/solution.py
@@ -10,8 +10,8 @@
 
 MESH = pl.DeviceIdType.MESH
 CORES = 2
-PIECES = (16, 16, 8, 4, 2)
-HOLD = ((0, 3300), (800, 0))
+PIECES = (32, 32, 16, 8, 4, 2)
+HOLD = ((0, 3000), (1000, 0))
 TILE = (16, 512)
 WAYS = (0, 1)
 F32, BF16 = jnp.float32, jnp.bfloat16
@@ -208,7 +208,7 @@
 
                 acc[...] = tiles(a, size, tile, acc[...])
 
-    squares[me] = acc[...]
+    squares[me] = jnp.sum(acc[...], axis=0, keepdims=True)
     for a in arrays:
         drain_blocks(sum_send.at[a], 3 * layers)
     for o in range(1, n):
@@ -221,7 +221,7 @@
     everyone = squares[0]
     for i in range(1, n):
         everyone = everyone + squares[i]
-    everyone = jnp.sum(jnp.sum(everyone, axis=1, keepdims=True), axis=0, keepdims=True)
+    everyone = jnp.sum(everyone, axis=1, keepdims=True)
     count = n * sum(ref.size for ref in m)
     factor = jnp.minimum(1.0, 0.5 * lax.rsqrt(everyone / count + 1e-30))
 
@@ -274,9 +274,9 @@
     for k, a, l in steps[:final]:
         for way in WAYS:
             here = new[a].at[way * half + l, block(a, source[way]), :]
-            there = last.at[way] if k == final - 1 else here
+            there, device = (here, side[way]) if k < final - 1 else (last.at[way], side[way] + 1 - 2 * core)
             pltpu.make_async_remote_copy(
-                src_ref=here, dst_ref=there, send_sem=ring_send.at[a], recv_sem=last_sem.at[k], **to(side[way])).start()
+                src_ref=here, dst_ref=there, send_sem=ring_send.at[a], recv_sem=last_sem.at[k], **to(device)).start()
     for k, a, l in steps:
         drain(second_sem.at[k], far[a].at[:, l])
         for way in WAYS:
@@ -286,8 +286,8 @@
     for way in WAYS:
         drain(tail_sem.at[way], new[a].at[way * half + l, block(a, mates((left_chip, right_chip)[way])), :])
     pair = CORES * height[a]
-    where = pl.ds(pl.multiple_of((left_chip + core * (right_chip - left_chip)) * pair, pair), pair)
-    to_tail = pltpu.make_async_copy(new[a].at[core * half + l, where, :], tail, tail_sem.at[3])
+    where = pl.ds(pl.multiple_of((right_chip + core * (left_chip - right_chip)) * pair, pair), pair)
+    to_tail = pltpu.make_async_copy(new[a].at[(1 - core) * half + l, where, :], tail, tail_sem.at[3])
     to_tail.start()
     for k, a, l in steps[: final - 1]:
         drain(last_sem.at[k], far[a].at[:, l])
@@ -309,7 +309,7 @@
 def solution(mesh):
     n = mesh.shape["dp"]
     chips = n // CORES
-    onward = [(i, (i // CORES + (1 if i % CORES == 0 else chips - 1)) % chips * CORES + 1 - i % CORES) for i in range(n)]
+    onward = [(i, (i // CORES + (chips - 1 if i % CORES == 0 else 1)) % chips * CORES + 1 - i % CORES) for i in range(n)]
     mates = [(i, i // CORES * CORES + 1 - i % CORES) for i in range(n)]
 
     def step(*arrays):
@@ -327,7 +327,7 @@
             [pltpu.VMEM((2, layers // 2, *b), BF16) for b in blocks]
             + [pltpu.VMEM((2, layers, *b), BF16) for b in blocks]
             + [pltpu.VMEM((layers, *b), BF16) for b in blocks]
-            + [pltpu.VMEM((layers, *blocks[fine]), BF16), pltpu.VMEM((8, 128), F32), pltpu.VMEM((n, 8, 128), F32)]
+            + [pltpu.VMEM((layers, *blocks[fine]), BF16), pltpu.VMEM((8, 128), F32), pltpu.VMEM((n, 1, 128), F32)]
             + [dma((7,)), dma((4,)), dma((len(PIECES),)), dma((2,))]
             + [dma((steps,)), dma((steps,)), dma((steps - 1 + len(PIECES),))]
             + [dma((3,)), dma((3,)), dma((3,)), dma((3,)), dma((3,)), dma((2,)), dma((4,))]
@@ -380,13 +380,13 @@
             def place(ref):
                 far_chip, core = far_rows(of_mate)
                 pair = CORES * rows
-                return ref.at[(CORES - core) * (layers // 2) - 1, pl.ds(pl.multiple_of(far_chip * pair, pair), pair), :]
+                return ref.at[(core + 1) * (layers // 2) - 1, pl.ds(pl.multiple_of(far_chip * pair, pair), pair), :]
 
             return place
 
         def from_last(of_mate):
             def place(ref):
-                far_chip, core = far_rows(of_mate)
+                far_chip, core = far_rows(not of_mate)
                 size = blocks[late][0]
                 return ref.at[layers // 2 - 1 :: layers // 2, pl.ds(pl.multiple_of((far_chip * CORES + core) * size, size), size), :]
 

time: 224 us -> 223 us (level)
    ppermute x1, starting transfers between devices: 3.3 us -> 0.09 us  [step(): own = lax.ppermute(tail, 'dp', onward)]
  transfers between devices with their start and end apart: 3 -> 3, of which waited for: 1 -> 2; matrix products, arithmetic and copies ran while one was open for 0% -> 0% of each run, Pallas kernels for 6% -> 6%
where the time goes in v8:
time: 223 us
  Pallas kernels  219 us (98%)
    pallas_call x1, Pallas kernels, step(): pl.pallas_call(functools.partial(kernel, n, fine), out_shape=[pltpu.VMEM(...  204 us
    pallas_call x3, Pallas kernels, write(): pl.pallas_call(body, out_shape=[jax.ShapeDtypeStruct(*out[i]) for i in wr...  15.1 us
  transfers between devices with their start and end apart: 3, of which 2 were waited for; matrix products, arithmetic and copies ran while one was open for 0% of the time, Pallas kernels for 6%

profile of v8, /device:TPU:113, one launch (start us, length us, event | category | flops | bytes accessed | tf_op | source)
XLA Modules:
  0.0 222.9 jit_solution(7111212988525801596)
XLA Ops:
  0.6 204.3 %shard_map.187 = (bf16[2,512,4096]{2,1,0:T(8,128)(2,1)S(1)}, bf16[2,512,4096]{2,1,0:T(8,128)(2,1)S(1)}, bf16[2,4096,512]{2,1,0:T(8,128)(2,1)S(1)}, f32[2,64,4096...) custom-call(bf16[1,2,512,4096]{3,2,1,0:T(8,128)(2,1)} %refs_0_.1, ...), custom_call_target="tpu_custom_call" | custom-call | tf_op jit(solution)/shard_map/pallas_call | solution.py:336
  205.0 0.1 collective-permute-start
  205.1 1.9 collective-permute-start.1
  207.0 11.7 %shard_map.188 = (bf16[2,512,4096]{2,1,0:T(8,128)(2,1)}, bf16[2,512,4096]{2,1,0:T(8,128)(2,1)}, bf16[2,4096,512]{2,1,0:T(8,128)(2,1)}, f32[2,64,4096]{2,1,0:T(8,...) custom-call(bf16[2,512,4096]{2,1,0:T(8,128)(2,1)S(1)} %get-tuple-elemen, ...), custom_call_target="tpu_custom_call" | custom-call | bytes 71303168 | tf_op jit(solution)/shard_map/pallas_call | solution.py:361
  218.7 0.6 collective-permute-done.refs_3_
  219.3 0.2 collective-permute-start.2
  219.5 0.0 collective-permute-done.1.refs_5_
  219.5 2.4 %shard_map.189 = (bf16[2,512,4096]{2,1,0:T(8,128)(2,1)}, bf16[2,4096,512]{2,1,0:T(8,128)(2,1)}, f32[2,512,512]{2,1,0:T(8,128)}) custom-call(bf16[2,512,4096]{2,1,0:T(8,128)(2,1)} %get-tuple-element.42.refs_0_, bf16[2,4096,512]{2,1,0:T(8,128)(2,1)} %get-tuple-element.45.refs_1_, ...), custom_call_target="tpu_custom_call", output_to_operand_aliasing={{0}: (0, {}), {1}: (1, {})} | custom-call | bytes 10485760 | tf_op jit(solution)/shard_map/pallas_call | solution.py:361
  221.9 0.1 collective-permute-done.2.refs_1_
  221.9 1.0 shard_map.190
Async XLA Ops:
  205.0 14.3 %collective-permute-start = (bf16[1024,512]{1,0:T(8,128)(2,1)S(1)}, bf16[1024,512]{1,0:T(8,128)(2,1)S(1)}, u32[]{:S(2)}, u32[]{:S(2)}) collective-permute-start(bf16[1024,512]{1,0:T(8,128)(2,1)S(1)} %get-tuple-element.43), channel_id=1, source_target_pairs={{0,7},{1,2},{2,1},{3,4},{4,3},{5,6},{6,5},{7,0},{8,15},{9,10},{10,... | collective-permute-start | bytes 3145736 | tf_op jit(solution)/shard_map/ppermute | solution.py:396
  205.1 14.4 %collective-permute-start.1 = (bf16[2,64,4096]{2,1,0:T(8,128)(2,1)S(1)}, bf16[2,64,4096]{2,1,0:T(8,128)(2,1)S(1)}, u32[]{:S(2)}, u32[]{:S(2)}) collective-permute-start(bf16[2,64,4096]{2,1,0:T(8,128)(2,1)S(1)} %get-tuple-element.48.refs_4_), channel_id=1, source_target_pairs={{0,1},{1,0},{2,3},{3,2},{4,5},{5,4},{6,7},{7,6},{8,9},{9,8},{10,11... | collective-permute-start | bytes 3145736 | tf_op jit(solution)/shard_map/ppermute | solution.py:397
  219.3 2.7 %collective-permute-start.2 = (bf16[1024,512]{1,0:T(8,128)(2,1)S(1)}, bf16[1024,512]{1,0:T(8,128)(2,1)S(1)}, u32[]{:S(2)}, u32[]{:S(2)}) collective-permute-start(bf16[1024,512]{1,0:T(8,128)(2,1)S(1)} %collective-permute-done.refs_3_), channel_id=1, source_target_pairs={{0,1},{1,0},{2,3},{3,2},{4,5},{5,4},{6,7},{7,6},{8,9},{9,8},{10,11... | collective-permute-start | bytes 3145736 | tf_op jit(solution)/shard_map/ppermute | solution.py:400

commit v9 on v8

--- a/solution.py
+++ b/solution.py
@@ -111,11 +111,12 @@
     barrier = pltpu.get_barrier_semaphore()
     for o in range(1, n):
         pl.semaphore_signal(barrier, inc=1, **to(lax.rem(me + o, n)))
-    for a in (fine, *arrays[:-1]):
-        term(0, a).start()
+    term(0, fine).start()
     to_stage(*staged[0]).wait()
     pl.semaphore_wait(barrier, n - 1)
     mate_head(*head[0]).start()
+    for a in arrays[:-1]:
+        term(0, a).start()
     to_stage(*staged[1]).wait()
     for piece in head[1:]:
         mate_head(*piece).start()
@@ -228,7 +229,7 @@
     def ring(way, a, index, layer, start, size, sem):
         here = new[a].at[layer, block(a, index, start, size), :]
         pltpu.make_async_remote_copy(
-            src_ref=here, dst_ref=here, send_sem=ring_send.at[a], recv_sem=sem, **to(side[way])).start()
+            src_ref=here, dst_ref=here, send_sem=ring_send.at[0], recv_sem=sem, **to(side[way])).start()
 
     def back(a, index, layer, start, size):
         here = new[a].at[layer, block(a, index, start, size), :]
@@ -276,7 +277,7 @@
             here = new[a].at[way * half + l, block(a, source[way]), :]
             there, device = (here, side[way]) if k < final - 1 else (last.at[way], side[way] + 1 - 2 * core)
             pltpu.make_async_remote_copy(
-                src_ref=here, dst_ref=there, send_sem=ring_send.at[a], recv_sem=last_sem.at[k], **to(device)).start()
+                src_ref=here, dst_ref=there, send_sem=ring_send.at[0], recv_sem=last_sem.at[k], **to(device)).start()
     for k, a, l in steps:
         drain(second_sem.at[k], far[a].at[:, l])
         for way in WAYS:
@@ -301,7 +302,7 @@
         blocks = (4 * layers - (4 if a == fine else 2 if a == steps[final - 1][1] else 0)) // half
         for sem in (back_send, back_sem):
             drain(sem.at[a], new[a].at[:half, pl.ds(0, blocks * height[a]), :])
-        drain_blocks(ring_send.at[a], 3 * layers - (2 if a == fine else 0))
+    drain_blocks(ring_send.at[0], 3 * layers * len(arrays) - 2)
     drain(last_sem.at[final - 1], last)
     drain(square_sem.at[0], squares.at[pl.ds(0, n - 1)])
 
@@ -330,7 +331,7 @@
             + [pltpu.VMEM((layers, *blocks[fine]), BF16), pltpu.VMEM((8, 128), F32), pltpu.VMEM((n, 1, 128), F32)]
             + [dma((7,)), dma((4,)), dma((len(PIECES),)), dma((2,))]
             + [dma((steps,)), dma((steps,)), dma((steps - 1 + len(PIECES),))]
-            + [dma((3,)), dma((3,)), dma((3,)), dma((3,)), dma((3,)), dma((2,)), dma((4,))]
+            + [dma((3,)), dma((3,)), dma((3,)), dma((3,)), dma((1,)), dma((2,)), dma((4,))]
         )
         late = [a for a in range(3) if a != fine][-1]
         *results, tail, last = pl.pallas_call(

time: 223 us -> 223 us (level)
  no operation moved by 1% of the time
where the time goes in v9:
time: 223 us
  Pallas kernels  219 us (98%)
    pallas_call x1, Pallas kernels, step(): pl.pallas_call(functools.partial(kernel, n, fine), out_shape=[pltpu.VMEM(...  204 us
    pallas_call x3, Pallas kernels, write(): pl.pallas_call(body, out_shape=[jax.ShapeDtypeStruct(*out[i]) for i in wr...  15.1 us
  transfers between devices with their start and end apart: 3, of which 2 were waited for; matrix products, arithmetic and copies ran while one was open for 0% of the time, Pallas kernels for 6%

profile of v9, /device:TPU:113, one launch (start us, length us, event | category | flops | bytes accessed | tf_op | source)
XLA Modules:
  0.0 222.9 jit_solution(5043231795497472909)
XLA Ops:
  0.6 204.3 %shard_map.187 = (bf16[2,512,4096]{2,1,0:T(8,128)(2,1)S(1)}, bf16[2,512,4096]{2,1,0:T(8,128)(2,1)S(1)}, bf16[2,4096,512]{2,1,0:T(8,128)(2,1)S(1)}, f32[2,64,4096...) custom-call(bf16[1,2,512,4096]{3,2,1,0:T(8,128)(2,1)} %refs_0_.1, ...), custom_call_target="tpu_custom_call" | custom-call | tf_op jit(solution)/shard_map/pallas_call | solution.py:337
  205.0 0.1 collective-permute-start
  205.1 1.9 collective-permute-start.1
  207.0 11.7 %shard_map.188 = (bf16[2,512,4096]{2,1,0:T(8,128)(2,1)}, bf16[2,512,4096]{2,1,0:T(8,128)(2,1)}, bf16[2,4096,512]{2,1,0:T(8,128)(2,1)}, f32[2,64,4096]{2,1,0:T(8,...) custom-call(bf16[2,512,4096]{2,1,0:T(8,128)(2,1)S(1)} %get-tuple-elemen, ...), custom_call_target="tpu_custom_call" | custom-call | bytes 71303168 | tf_op jit(solution)/shard_map/pallas_call | solution.py:362
  218.7 0.6 collective-permute-done.refs_3_
  219.3 0.2 collective-permute-start.2
  219.5 0.0 collective-permute-done.1.refs_5_
  219.5 2.4 %shard_map.189 = (bf16[2,512,4096]{2,1,0:T(8,128)(2,1)}, bf16[2,4096,512]{2,1,0:T(8,128)(2,1)}, f32[2,512,512]{2,1,0:T(8,128)}) custom-call(bf16[2,512,4096]{2,1,0:T(8,128)(2,1)} %get-tuple-element.42.refs_0_, bf16[2,4096,512]{2,1,0:T(8,128)(2,1)} %get-tuple-element.45.refs_1_, ...), custom_call_target="tpu_custom_call", output_to_operand_aliasing={{0}: (0, {}), {1}: (1, {})} | custom-call | bytes 10485760 | tf_op jit(solution)/shard_map/pallas_call | solution.py:362
  221.8 0.1 collective-permute-done.2.refs_1_
  221.9 1.0 shard_map.190
Async XLA Ops:
  205.0 14.3 %collective-permute-start = (bf16[1024,512]{1,0:T(8,128)(2,1)S(1)}, bf16[1024,512]{1,0:T(8,128)(2,1)S(1)}, u32[]{:S(2)}, u32[]{:S(2)}) collective-permute-start(bf16[1024,512]{1,0:T(8,128)(2,1)S(1)} %get-tuple-element.43), channel_id=1, source_target_pairs={{0,7},{1,2},{2,1},{3,4},{4,3},{5,6},{6,5},{7,0},{8,15},{9,10},{10,... | collective-permute-start | bytes 3145736 | tf_op jit(solution)/shard_map/ppermute | solution.py:397
  205.1 14.4 %collective-permute-start.1 = (bf16[2,64,4096]{2,1,0:T(8,128)(2,1)S(1)}, bf16[2,64,4096]{2,1,0:T(8,128)(2,1)S(1)}, u32[]{:S(2)}, u32[]{:S(2)}) collective-permute-start(bf16[2,64,4096]{2,1,0:T(8,128)(2,1)S(1)} %get-tuple-element.48.refs_4_), channel_id=1, source_target_pairs={{0,1},{1,0},{2,3},{3,2},{4,5},{5,4},{6,7},{7,6},{8,9},{9,8},{10,11... | collective-permute-start | bytes 3145736 | tf_op jit(solution)/shard_map/ppermute | solution.py:398
  219.3 2.7 %collective-permute-start.2 = (bf16[1024,512]{1,0:T(8,128)(2,1)S(1)}, bf16[1024,512]{1,0:T(8,128)(2,1)S(1)}, u32[]{:S(2)}, u32[]{:S(2)}) collective-permute-start(bf16[1024,512]{1,0:T(8,128)(2,1)S(1)} %collective-permute-done.refs_3_), channel_id=1, source_target_pairs={{0,1},{1,0},{2,3},{3,2},{4,5},{5,4},{6,7},{7,6},{8,9},{9,8},{10,11... | collective-permute-start | bytes 3145736 | tf_op jit(solution)/shard_map/ppermute | solution.py:401
